TPU v7x, 256 devices: a whole 4x4x8 slice. The times are simulated.
256 devices in a mesh: dp: 8 (over x, core), expert: 32 (over y, z).
Axes of the slice: x: 4, y: 4, z: 8, core: 2. Of those that a mesh axis runs over, the one named last changes fastest.
Arguments:
- queries: bfloat16 [2048, 16, 3072], P('expert', 'dp'), may hold values from -256 to 256
- key_nope: bfloat16 [2048, 16, 2048], P('expert', 'dp'), may hold values from -4 to 4
- key_rope: bfloat16 [2048, 16, 64], P('expert', 'dp'), may hold values from -4 to 4
- values: bfloat16 [2048, 16, 2048], P('expert', 'dp'), may hold values from -6 to 6
- residual: bfloat16 [2048, 16, 2048], P('expert', 'dp'), may hold values from -6 to 6
- segments: int32 [16, 2048], P('dp'), may hold values from 0 to 1, never falling along the last dimension, each value on 1 to 1536 neighbouring positions
- out_proj: bfloat16 [2048, 2048], P(('dp', 'expert')), may hold values from -0.125 to 0.125
- norm_gain: bfloat16 [2048], replicated, may hold values from 0.5 to 1.5
- expert_gate: bfloat16 [32, 2048, 704], P('expert'), may hold values from -0.125 to 0.125
- expert_up: bfloat16 [32, 2048, 704], P('expert'), may hold values from -0.125 to 0.125
- expert_down: bfloat16 [32, 704, 2048], P('expert'), may hold values from -0.21875 to 0.21875
- routes: int32 [8, 32, 128, 6], P('dp', 'expert'), may hold values from 0 to 31, all different within a row; in each aligned block of 128 rows (0 to 127, 128 to 255, ..., all dimensions but the last counted through in order) at most 36 rows name the same one
- route_weights: float32 [8, 32, 128, 6], P('dp', 'expert'), may hold values from 0.1 to 0.6
Outputs:
- layer_out: bfloat16 [2048, 16, 2048], P('expert', 'dp')
Inputs may be any that keep to these rules, and one draw needn't show every extreme that they name: `routes`: each row names 6 different experts; within the rows of one device no expert is named more than 36 times.
All inputs are finite; a program needn't handle non-finite values.
Results may differ from a plain program's by a relative error of at most 0.0049.
Values may be sent and summed in bfloat16 or wider, within the bound.
A program may use at most 128 MiB of HBM per device.

v0:
```python
import jax
import jax.numpy as jnp
from jax import lax
from jax.sharding import PartitionSpec as P

HEADS = 16
NOPE = 128
ROPE = 64
V_DIM = 128
TOP = 6


EPSILON = 1e-06
QUERY_BLOCK = 512


def side_by_side(arrays, axis, split_dim, concat_dim, along):
    widths = [a.shape[along] for a in arrays]
    both = jnp.concatenate(arrays, axis=along)
    result = lax.all_to_all(both, axis, split_axis=split_dim, concat_axis=concat_dim, tiled=True)
    return tuple(jnp.split(result, [sum(widths[:k]) for k in range(1, len(widths))], axis=along))


def feed_forward(rows, gate_matrix, up_matrix, down_matrix):
    gate_part = jnp.dot(rows, gate_matrix, preferred_element_type=jnp.float32)
    up_part = jnp.dot(rows, up_matrix, preferred_element_type=jnp.float32)
    activated = (jax.nn.silu(gate_part) * up_part).astype(jnp.bfloat16)
    return jnp.dot(activated, down_matrix, preferred_element_type=jnp.float32).astype(jnp.bfloat16)


def attend_items(query_items, key_items, value_items, segment_items):
    length, count_items, qk_width = query_items.shape
    block_rows = QUERY_BLOCK
    score_scale = qk_width ** (-0.5)
    key_positions = jnp.arange(length, dtype=jnp.int32)

    def one_block(block_index):
        first_row = block_index * block_rows
        query_block = lax.dynamic_slice_in_dim(query_items, first_row, block_rows, 0)
        scores = (
            jnp.einsum("qid,kid->iqk", query_block, key_items, preferred_element_type=jnp.float32)
            * score_scale
        )
        row_positions = first_row + jnp.arange(block_rows, dtype=jnp.int32)
        row_segments = lax.dynamic_slice_in_dim(segment_items, first_row, block_rows, 1)
        allowed = (row_positions[None, :, None] >= key_positions[None, None, :]) & (
            row_segments[:, :, None] == segment_items[:, None, :]
        )
        scores = jnp.where(allowed, scores, -jnp.inf)
        row_peak = jnp.max(scores, axis=2, keepdims=True)
        raised = jnp.exp(scores - row_peak)
        weights = (raised / jnp.sum(raised, axis=2, keepdims=True)).astype(jnp.bfloat16)
        return jnp.einsum(
            "iqk,kid->qid", weights, value_items, preferred_element_type=jnp.float32
        ).astype(jnp.bfloat16)

    blocks = lax.map(one_block, jnp.arange(length // block_rows, dtype=jnp.int32))
    return blocks.reshape(length, count_items, value_items.shape[2])


def body(
    queries,
    key_nope,
    key_rope,
    values,
    residual,
    segments,
    out_proj,
    norm_gain,
    expert_gate,
    expert_up,
    expert_down,
    routes,
    route_weights,
):
    half_rows, stream_count, query_width = queries.shape
    model_width = residual.shape[2]
    token_rows = half_rows * stream_count
    pair_count = token_rows * TOP
    expert_count = lax.axis_size("expert")
    item_count = stream_count * HEADS // expert_count
    key_heads = jnp.concatenate(
        [
            key_nope.reshape(half_rows, stream_count, HEADS, NOPE),
            jnp.broadcast_to(key_rope[:, :, None, :], (half_rows, stream_count, HEADS, ROPE)),
        ],
        axis=3,
    )
    query_items = queries.reshape(half_rows, stream_count * HEADS, NOPE + ROPE)
    key_items = key_heads.reshape(half_rows, stream_count * HEADS, NOPE + ROPE)
    value_items = values.reshape(half_rows, stream_count * HEADS, V_DIM)
    query_all, key_all, value_all = side_by_side(
        (query_items, key_items, value_items), "expert", 1, 0, 2
    )
    item_ids = lax.axis_index("expert") * item_count + jnp.arange(item_count, dtype=jnp.int32)
    stream_ids = item_ids // HEADS
    selector = (stream_ids[:, None] == jnp.arange(stream_count, dtype=jnp.int32)[None, :]).astype(
        jnp.int32
    )
    segment_items = jnp.sum(selector[:, :, None] * segments[None, :, :], axis=1)
    attended_items = attend_items(query_all, key_all, value_all, segment_items)
    attended_back = lax.all_to_all(
        attended_items, "expert", split_axis=0, concat_axis=1, tiled=True
    )
    attn_rows = attended_back.reshape(token_rows, HEADS * V_DIM)
    projected = jnp.dot(
        attn_rows,
        lax.all_gather(out_proj, ("dp", "expert"), axis=0, tiled=True),
        preferred_element_type=jnp.float32,
    )
    hidden = residual.reshape(token_rows, model_width).astype(jnp.float32) + projected
    mean_square = jnp.mean(hidden * hidden, axis=1, keepdims=True)
    normed = (hidden * lax.rsqrt(mean_square + EPSILON) * norm_gain.astype(jnp.float32)).astype(
        jnp.bfloat16
    )
    capacity = min(token_rows, max(2, token_rows * TOP * 3 // (2 * expert_count)))
    flat_routes = routes.reshape(pair_count)
    matches = (flat_routes[:, None] == jnp.arange(expert_count, dtype=jnp.int32)[None, :]).astype(
        jnp.int32
    )
    earlier = jnp.cumsum(matches, axis=0) - matches
    slot_rank = jnp.sum(earlier * matches, axis=1)
    target = flat_routes * capacity + slot_rank
    pair_ids = jnp.arange(pair_count, dtype=jnp.int32)
    slot_source = (
        jnp.full((expert_count * capacity,), pair_count, jnp.int32).at[target].set(pair_ids)
    )
    slot_live = slot_source < pair_count
    slot_rows = normed[jnp.minimum(slot_source, pair_count - 1) // TOP]
    outgoing = jnp.where(slot_live[:, None], slot_rows, jnp.zeros_like(slot_rows)).reshape(
        expert_count, capacity, model_width
    )
    gate_matrix = expert_gate[0]
    up_matrix = expert_up[0]
    down_matrix = expert_down[0]
    arrived = lax.all_to_all(outgoing, "expert", split_axis=0, concat_axis=0, tiled=True)
    source_count, slot_count, width = arrived.shape
    flat_rows = arrived.reshape(source_count * slot_count, width)
    results = feed_forward(flat_rows, gate_matrix, up_matrix, down_matrix)
    returned = lax.all_to_all(
        results.reshape(source_count, slot_count, width),
        "expert",
        split_axis=0,
        concat_axis=0,
        tiled=True,
    )
    pair_outputs = returned.reshape(expert_count * capacity, model_width)[target]
    weighted = route_weights.reshape(pair_count, 1) * pair_outputs.astype(jnp.float32)
    routed_sum = jnp.sum(weighted.reshape(token_rows, TOP, model_width), axis=1)
    layer_out = (hidden + routed_sum).astype(jnp.bfloat16)
    return layer_out.reshape(half_rows, stream_count, model_width)


def solution(mesh):
    return jax.shard_map(
        body,
        mesh=mesh,
        in_specs=(
            P("expert", "dp", None),
            P("expert", "dp", None),
            P("expert", "dp", None),
            P("expert", "dp", None),
            P("expert", "dp", None),
            P("dp", None),
            P(("dp", "expert"), None),
            P(),
            P("expert", None, None),
            P("expert", None, None),
            P("expert", None, None),
            P("dp", "expert", None, None),
            P("dp", "expert", None, None),
        ),
        out_specs=P("expert", "dp", None),
        check_vma=False,
    )
```

profile of v0, /device:TPU:2, one launch (start us, length us, event | category | flops | bytes accessed | tf_op | source)
XLA Modules:
  0.0 490.3 jit_solution(3616979973672763825)
XLA Ops:
  7.3 3.5 reshape.177
  10.8 1.4 concatenate.10
  12.2 2.2 reshape.178
  15.2 2.3 pad_maximum_fusion
  17.5 2.6 copy.45
  20.1 11.7 %all-to-all-start = ((bf16[64,32,512]{2,0,1:T(8,128)(2,1)}), bf16[64,32,512]{2,0,1:T(8,128)(2,1)}, u32[]{:S(2)}, u32[]{:S(2)}) async-start(bf16[64,32,512]{2,0,1:T(8,128)(2,1)} %copy.45), calls=%async_computation | async-start | bytes 4194304 | tf_op jit(solution)/shard_map/all_to_all | solution.py:20
  32.3 1.2 reshape.186
  33.5 1.7 reduce-window.6
  35.7 49.4 %all-to-all-done = bf16[64,32,512]{2,0,1:T(8,128)(2,1)} async-done(((bf16[64,32,512]{2,0,1:T(8,128)(2,1)}), bf16[64,32,512]{2,0,1:T(8,128)(2,1)}, u32[]{:S(2)}, u32[]{:S(2)}) %all-to-all-start) | async-done | bytes 2097184 | tf_op jit(solution)/shard_map/all_to_all | solution.py:20
  85.0 1.1 split.14
  86.1 3.6 fusion.27
  89.7 2.2 copy.46
  91.9 2.2 copy.47
  94.1 24.3 %while.11 = (s32[]{:T(128)}, bf16[4,512,1,128]{3,1,2,0:T(8,128)(2,1)}, s32[4]{0:T(128)S(1)}, s32[1,2048]{1,0:T(1,128)S(1)}, bf16[2048,1,192]{0,2,1:T(8,128)(2,1)...) while((s32[]{:T(128)}, ...), condition=%wide.region_4.5_spmd.clone, body=%wide.region_1.4_spmd.clone.sunk | while | flops 682688000 | bytes 14250675 | solution.py:57
  95.4 2.6 fusion.38
  98.7 1.5 fusion.40
  101.4 2.6 fusion.38
  104.7 1.5 fusion.40
  107.5 2.6 fusion.38
  110.8 1.5 fusion.40
  113.6 2.6 fusion.38
  116.9 1.5 fusion.40
  119.0 2.1 reduce.10
  122.0 5.5 %all-to-all-start.1 = ((bf16[32,2,4096]{2,1,0:T(2,128)(2,1)}), bf16[32,2,4096]{2,1,0:T(2,128)(2,1)S(1)}, u32[]{:S(2)}, u32[]{:S(2)}) async-start(bf16[32,2,4096]{2,1,0:T(2,128)(2,1)} %reshape.220), calls=%async_computation.1 | async-start | bytes 1048576 | tf_op jit(solution)/shard_map/all_to_all | solution.py:102
  129.4 3.6 scatter_custom_fusion
  133.1 11.8 %all-to-all-done.1 = bf16[32,2,4096]{2,1,0:T(2,128)(2,1)S(1)} async-done(((bf16[32,2,4096]{2,1,0:T(2,128)(2,1)}), bf16[32,2,4096]{2,1,0:T(2,128)(2,1)S(1)}, u32[]{:S(2)}, u32[]{:S(2)}) %all-to-all-start.1) | async-done | bytes 524320 | tf_op jit(solution)/shard_map/all_to_all | solution.py:102
  144.9 1.8 reshape.221
  146.7 1.3 copy.56
  148.0 1.1 copy.49
  149.2 1.3 reshape.180
  150.5 5.0 %multiply_reduce_fusion.1 = (f32[128]{0:T(128)S(1)}, f32[128,2048]{1,0:T(8,128)S(1)}) fusion(f32[128,2048]{1,0:T(8,128)} %reshape.186, bf16[128,2048]{1,0:T(8,128)(2,1)S(1)} %reshape.180, bf16[2048,2048]{1,0:T(8,128)(2,1)} %all-gather.2.cloned.1.call-done), kind=kOutput, calls=%fused_computation.34 | convolution fusion | flops 1074528128 | bytes 11010560 | tf_op jit(solution)/shard_map/dot_general | solution.py:106
  155.5 1.0 copy-done.1
  156.6 6.1 %gather_fusion = bf16[1152,2048]{1,0:T(8,128)(2,1)} fusion(bf16[128,2048]{1,0:T(8,128)(2,1)S(1)} %multiply_convert_fusion, s32[2048]{0:T(1024)S(1)} %pad_clamp_fusion), kind=kCustom, calls=%fused_computation | custom fusion | bytes 9441792 | tf_op jit(solution)/shard_map/gather | solution.py:129
  162.7 7.2 %gather.9 = bf16[32,36,2048]{2,1,0:T(8,128)(2,1)} reshape(bf16[1152,2048]{1,0:T(8,128)(2,1)} %gather_fusion) | data formatting | bytes 9437184 | tf_op jit(solution)/shard_map/gather | solution.py:129
  169.9 2.9 broadcast_select_fusion
  172.8 123.9 %all_to_all.43 = bf16[32,36,2048]{2,1,0:T(8,128)(2,1)} all-to-all(bf16[32,36,2048]{2,1,0:T(8,128)(2,1)S(1)} %broadcast_select_fusion), channel_id=1, replica_groups=mesh['dp'=8,'expert'=32] {'expert'}, dimensions={0} | all-to-all | bytes 9437184 | tf_op jit(solution)/shard_map/all_to_all | solution.py:136
  296.7 7.3 %reshape.182 = bf16[1152,2048]{1,0:T(8,128)(2,1)} reshape(bf16[32,36,2048]{2,1,0:T(8,128)(2,1)} %all_to_all.43) | data formatting | bytes 9437184 | tf_op jit(solution)/shard_map/reshape | solution.py:138
  304.0 7.3 %fusion.16 = f32[1152,704]{0,1:T(8,128)S(1)} fusion(bf16[1152,2048]{1,0:T(8,128)(2,1)} %reshape.182, bf16[1,2048,704]{1,2,0:T(8,128)(2,1)} %param.23), kind=kOutput, calls=%fused_computation.28 | convolution fusion | flops 3321888768 | bytes 10846208 | tf_op jit(solution)/shard_map/dot_general | solution.py:25
  311.3 4.0 fusion.13
  315.4 5.6 %convolution_convert_fusion = bf16[1152,2048]{1,0:T(8,128)(2,1)} fusion(bf16[1152,704]{0,1:T(8,128)(2,1)S(1)} %fusion.13, bf16[1,704,2048]{2,1,0:T(8,128)(2,1)S(1)} %copy-done), kind=kOutput, calls=%fused_computation.22 | convolution fusion | flops 3324248064 | bytes 9224192 | tf_op jit(solution)/shard_map/dot_general | solution.py:28
  320.9 7.3 %reshape.183 = bf16[32,36,2048]{2,1,0:T(8,128)(2,1)} reshape(bf16[1152,2048]{1,0:T(8,128)(2,1)} %convolution_convert_fusion) | data formatting | bytes 9437184 | tf_op jit(solution)/shard_map/reshape | solution.py:141
  328.2 5.4 %all-to-all-start.3 = ((bf16[32,36,2048]{2,1,0:T(8,128)(2,1)}), bf16[32,36,2048]{2,1,0:T(8,128)(2,1)}, u32[]{:S(2)}, u32[]{:S(2)}) async-start(bf16[32,36,2048]{2,1,0:T(8,128)(2,1)} %reshape.183), calls=%async_computation.3 | async-start | bytes 10485760 | tf_op jit(solution)/shard_map/all_to_all | solution.py:140
  333.7 117.9 %all-to-all-done.3 = bf16[32,36,2048]{2,1,0:T(8,128)(2,1)} async-done(((bf16[32,36,2048]{2,1,0:T(8,128)(2,1)}), bf16[32,36,2048]{2,1,0:T(8,128)(2,1)}, u32[]{:S(2)}, u32[]{:S(2)}) %all-to-all-start.3) | async-done | bytes 4718624 | tf_op jit(solution)/shard_map/all_to_all | solution.py:140
  451.6 7.3 %reshape.184 = bf16[1152,2048]{1,0:T(8,128)(2,1)} reshape(bf16[32,36,2048]{2,1,0:T(8,128)(2,1)} %all-to-all-done.3) | data formatting | bytes 9437184 | tf_op jit(solution)/shard_map/reshape | solution.py:147
  458.9 10.0 %gather_fusion.1 = bf16[768,2048]{1,0:T(8,128)(2,1)} fusion(bf16[1152,2048]{1,0:T(8,128)(2,1)} %reshape.184, s32[1024]{0:T(1024)S(1)} %pad_clamp_fusion.1), kind=kCustom, calls=%fused_computation.1 | custom fusion | bytes 6294528 | tf_op jit(solution)/shard_map/gather | solution.py:147
  469.0 6.5 %reshape.187 = f32[128,6,2048]{2,1,0:T(8,128)} reshape(bf16[768,2048]{1,0:T(8,128)(2,1)} %gather_fusion.1) | data formatting | bytes 9437184 | tf_op jit(solution)/shard_map/convert_element_type | solution.py:148
  475.5 6.7 %multiply_reduce_fusion = f32[128,2048]{1,0:T(8,128)S(1)} fusion(f32[128,6,2048]{2,1,0:T(8,128)} %reshape.187, f32[128,6]{1,0:T(8,128)S(1)} %bitcast.100), kind=kLoop, calls=%fused_computation.21 | loop fusion | flops 2883584 | bytes 7343104 | tf_op jit(solution)/shard_map/reduce_sum | solution.py:149
  482.3 1.1 reshape.185
  (67 shorter events, 11.5 us)
Async XLA Ops:
  6.5 308.8 %copy-start = (bf16[1,704,2048]{2,1,0:T(8,128)(2,1)S(1)}, bf16[1,704,2048]{2,1,0:T(8,128)(2,1)}, u32[]{:S(2)}) copy-start(bf16[1,704,2048]{2,1,0:T(8,128)(2,1)} %param.25) | copy-start | bytes 8650756
  6.5 143.9 %all-gather.2.cloned.1.call-start = ((), (), s32[]{:S(2)}) async-start(), calls=%async_computation.4 | async-start | bytes 8421376 | tf_op jit(solution)/shard_map/all_gather | solution.py:108
  17.5 14.4 %copy-start.6 = (s32[1,1,128,6]{2,1,3,0:T(1,128)S(1)}, s32[1,1,128,6]{2,1,3,0:T(1,128)}, u32[]{:S(2)}) copy-start(s32[1,1,128,6]{2,1,3,0:T(1,128)} %param.26) | copy-start | bytes 9220
  17.5 14.8 %copy-start.4 = (bf16[64,2,2048]{2,1,0:T(2,128)(2,1)S(1)}, bf16[64,2,2048]{2,1,0:T(2,128)(2,1)}, u32[]{:S(2)}) copy-start(bf16[64,2,2048]{2,1,0:T(2,128)(2,1)} %param.19) | copy-start | bytes 1572868
  17.5 16.0 %copy-start.7 = (bf16[2048]{0:T(1024)(128)(2,1)S(1)}, bf16[2048]{0:T(1024)(128)(2,1)}, u32[]{:S(2)}) copy-start(bf16[2048]{0:T(1024)(128)(2,1)} %param.22) | copy-start | bytes 12292
  20.1 15.5 %copy-start.5 = (s32[2,2048]{1,0:T(2,128)S(1)}, s32[2,2048]{1,0:T(2,128)}, u32[]{:S(2)}) copy-start(s32[2,2048]{1,0:T(2,128)} %param.20) | copy-start | bytes 49156
  20.1 64.9 %all-to-all-start = ((bf16[64,32,512]{2,0,1:T(8,128)(2,1)}), bf16[64,32,512]{2,0,1:T(8,128)(2,1)}, u32[]{:S(2)}, u32[]{:S(2)}) async-start(bf16[64,32,512]{2,0,1:T(8,128)(2,1)} %copy.45), calls=%async_computation | async-start | bytes 4194304 | tf_op jit(solution)/shard_map/all_to_all | solution.py:20
  122.0 22.9 %all-to-all-start.1 = ((bf16[32,2,4096]{2,1,0:T(2,128)(2,1)}), bf16[32,2,4096]{2,1,0:T(2,128)(2,1)S(1)}, u32[]{:S(2)}, u32[]{:S(2)}) async-start(bf16[32,2,4096]{2,1,0:T(2,128)(2,1)} %reshape.220), calls=%async_computation.1 | async-start | bytes 1048576 | tf_op jit(solution)/shard_map/all_to_all | solution.py:102
  155.4 1.0 copy-start.1
  304.0 7.3 %copy-start.3 = (bf16[1152,2048]{1,0:T(8,128)(2,1)S(1)}, bf16[1152,2048]{1,0:T(8,128)(2,1)}, u32[]{:S(2)}) copy-start(bf16[1152,2048]{1,0:T(8,128)(2,1)} %reshape.182) | copy-start | bytes 14155780
  304.0 7.3 %copy-start.9 = (bf16[1,2048,704]{1,2,0:T(8,128)(2,1)S(1)}, bf16[1,2048,704]{1,2,0:T(8,128)(2,1)}, u32[]{:S(2)}) copy-start(bf16[1,2048,704]{1,2,0:T(8,128)(2,1)} %param.24) | copy-start | bytes 8650756
  328.2 5.4 %copy-start.8 = (f32[1,1,128,6]{2,1,3,0:T(1,128)S(1)}, f32[1,1,128,6]{2,1,3,0:T(1,128)}, u32[]{:S(2)}) copy-start(f32[1,1,128,6]{2,1,3,0:T(1,128)} %param.27) | copy-start | bytes 9220
  328.2 123.4 %all-to-all-start.3 = ((bf16[32,36,2048]{2,1,0:T(8,128)(2,1)}), bf16[32,36,2048]{2,1,0:T(8,128)(2,1)}, u32[]{:S(2)}, u32[]{:S(2)}) async-start(bf16[32,36,2048]{2,1,0:T(8,128)(2,1)} %reshape.183), calls=%async_computation.3 | async-start | bytes 10485760 | tf_op jit(solution)/shard_map/all_to_all | solution.py:140
  475.5 6.7 %copy-start.2 = (f32[128,2048]{1,0:T(8,128)S(1)}, f32[128,2048]{1,0:T(8,128)}, u32[]{:S(2)}) copy-start(f32[128,2048]{1,0:T(8,128)} %copy-done.1) | copy-start | bytes 3145732
Sparse Core Ops, SparseCore 0:
  11.0 128.0 all-gather.1
where the time goes:
time: 492 us; the launch traced here: 490 us
  waiting for transfers between devices  180 us (37%)
  blocking collectives  124 us (25%)
  local copies, waits for them, and re-layouts  90.1 us (18%)
  matrix products  38.3 us (8%)
  starting transfers between devices  22.7 us (5%)
  other arithmetic  19.1 us (4%)
  between operations  13.7 us (3%)
    all_to_all x1, blocking collectives, body(): lax.all_to_all(outgoing, 'expert', split_axis=0, concat_axis=0, tiled=True)  124 us
    all_to_all x1, waiting for transfers between devices, body(): lax.all_to_all(results.reshape(source_count, slot_count, width), 'expert'...  118 us
    all_to_all x1, waiting for transfers between devices, side_by_side(): lax.all_to_all(both, axis, split_axis=split_dim, concat_axis=concat_dim,...  49.4 us
    gather x2, local copies, waits for them, and re-layouts, body(): slot_rows = normed[jnp.minimum(slot_source, pair_count - 1) // TOP]  13.3 us
    all_to_all x1, waiting for transfers between devices, body(): lax.all_to_all(attended_items, 'expert', split_axis=0, concat_axis=1, til...  11.8 us
    all_to_all x1, starting transfers between devices, side_by_side(): lax.all_to_all(both, axis, split_axis=split_dim, concat_axis=concat_dim,...  11.7 us
    dot_general x4, matrix products, one_block(): jnp.einsum('qid,kid->iqk', query_block, key_items, preferred_element_type...  10.3 us
    gather x1, local copies, waits for them, and re-layouts, body(): returned.reshape(expert_count * capacity, model_width)[target]  10 us
  transfers between devices with their start and end apart: 4, of which 3 were waited for; matrix products, arithmetic and copies ran while one was open for 13% of the time, Pallas kernels for 0%

commit v1 on v0

v1 whole, which is shorter than its diff:
```python
import functools

import jax
import jax.numpy as jnp
from jax import lax
from jax.experimental import pallas as pl
from jax.experimental.pallas import tpu as pltpu
from jax.sharding import Mesh, PartitionSpec as P

MESH = pl.DeviceIdType.MESH
DP = ("x", "core")
EXPERT = ("y", "z")

HEADS = 16
NOPE = 128
ROPE = 64
V_DIM = 128
TOP = 6


EPSILON = 1e-06
QUERY_BLOCK = 512


def side_by_side(arrays, axis, split_dim, concat_dim, along):
    widths = [a.shape[along] for a in arrays]
    both = jnp.concatenate(arrays, axis=along)
    result = lax.all_to_all(both, axis, split_axis=split_dim, concat_axis=concat_dim, tiled=True)
    return tuple(jnp.split(result, [sum(widths[:k]) for k in range(1, len(widths))], axis=along))


def moe_kernel(axis_size, x_ref, hid_ref, wt_ref, wi_hbm, wd_hbm, out_ref,
               xbuf, acc, act, wi, wd, rbuf, lbuf, start_sem, send_sem, recv_sem, wsem):
    n = axis_size
    half_n = n // 2
    z = lax.axis_index("z")
    right = {"z": lax.rem(z + 1, n)}
    left = {"z": lax.rem(z + n - 1, n)}
    rows = x_ref.shape[0]
    half = rows // 2
    pieces, count, depth, ff = wi_hbm.shape[:3] + (wi_hbm.shape[3] // 2,)
    sent = 2 * half_n - 1

    def slot(d):
        return lax.rem(z + 2 * n - d, n)

    def part(c):
        return pl.ds(pl.multiple_of(c * half, half), half)

    def fetch(k, carry):
        for i in range(pieces):
            span = pl.ds(i * depth, depth)
            pltpu.make_async_copy(wi_hbm.at[i, k], wi.at[k, span], wsem.at[k, 0]).start()
            pltpu.make_async_copy(wd_hbm.at[i, k], wd.at[k, :, span], wsem.at[k, 1]).start()
        return carry

    lax.fori_loop(0, count, fetch, 0)

    barrier = pltpu.get_barrier_semaphore()
    for neighbour in (left, right):
        pl.semaphore_signal(barrier, inc=1, device_id=neighbour, device_id_type=MESH)
    pl.semaphore_wait(barrier, 2)

    def gather_copy(j, way):
        d = j // 2
        c = lax.rem(j + way, 2)
        source = slot(d) if way == 0 else slot(n - d)
        return pltpu.make_async_remote_copy(
            src_ref=xbuf.at[source, part(c)],
            dst_ref=xbuf.at[source, part(c)],
            send_sem=send_sem.at[way, j],
            recv_sem=recv_sem.at[way, j],
            device_id=right if way == 0 else left,
            device_id_type=MESH,
        )

    def gather_arrival(j, way):
        d = j // 2 + 1
        c = lax.rem(j + way, 2)
        source = slot(d) if way == 0 else slot(n - d)
        return pltpu.make_async_remote_copy(
            src_ref=xbuf.at[source, part(c)],
            dst_ref=xbuf.at[source, part(c)],
            send_sem=send_sem.at[way, j],
            recv_sem=recv_sem.at[way, j],
            device_id=right if way == 0 else left,
            device_id_type=MESH,
        )

    own_copy = pltpu.make_async_copy(x_ref, xbuf.at[z], start_sem)
    own_copy.start()
    own_copy.wait()
    for j in range(2):
        for way in range(2):
            gather_copy(j, way).start()

    def pass_on(j):
        for way in range(2):
            gather_arrival(j, way).wait_recv()

        @pl.when(j + 2 < sent)
        def _():
            for way in range(2):
                gather_copy(j + 2, way).start()

    lanes = lax.broadcasted_iota(jnp.int32, (1, wt_ref.shape[2]), 1)
    main = ff // 128 * 128
    rest = ff - main
    cuts = [(a, min(a + 256, main)) for a in range(0, main, 256)]
    width = xbuf.shape[2]

    def gate_up(slots, k):
        x = jnp.concatenate([xbuf[s] for s in slots], axis=0) if len(slots) > 1 else xbuf[slots[0]]
        wrow = jnp.concatenate([wt_ref[s] for s in slots], axis=0) if len(slots) > 1 else wt_ref[slots[0]]
        scale = jnp.sum(jnp.where(lanes == k, wrow, 0.0), axis=1, keepdims=True)
        m = x.shape[0]

        def product(lo, hi):
            return jnp.dot(x, wi[k, :, lo:hi], preferred_element_type=jnp.float32)

        def put(lo, hi, g, u):
            a = g / (1.0 + jnp.exp(-g)) * u * scale
            act[k, 0:m, lo:hi] = a.astype(jnp.bfloat16)

        start = main + 2 * rest
        for lo, hi in cuts:
            if hi == main and rest:
                both = product(lo, start)
                put(lo, hi, both[:, :hi - lo], product(start + lo, start + hi))
                put(main, ff, both[:, hi - lo:hi - lo + rest], both[:, hi - lo + rest:])
            else:
                put(lo, hi, product(lo, hi), product(start + lo, start + hi))

    def down(slots):
        m = rows * len(slots)

        def columns(q, carry):
            span = pl.ds(pl.multiple_of(q * 512, min(512, width)), min(512, width))
            y = jnp.dot(act[0, 0:m, :], wd[0, :, span], preferred_element_type=jnp.float32)
            for k in range(1, count):
                y += jnp.dot(act[k, 0:m, :], wd[k, :, span], preferred_element_type=jnp.float32)
            y = y.astype(jnp.bfloat16)
            for i, s in enumerate(slots):
                acc[s, :, span] = y[i * rows:(i + 1) * rows]
            return carry

        lax.fori_loop(0, max(1, width // 512), columns, 0)

    def fetched(k, which):
        whole = (wi, wd)[which].at[k]
        pltpu.make_async_copy(whole, whole, wsem.at[k, which]).wait()

    def own_step(k, carry):
        fetched(k, 0)
        gate_up([z], k)

        @pl.when(k == 1)
        def _():
            pass_on(0)

        return carry

    lax.fori_loop(0, count, own_step, 0)
    for k in range(count):
        fetched(k, 1)
    down([z])

    def pair_step(p, carry):
        pass_on(2 * p - 1)
        slots = [slot(p), slot(n - p)]

        def one(k, inner):
            gate_up(slots, k)

            @pl.when(k == 1)
            def _():
                pass_on(2 * p)

            return inner

        lax.fori_loop(0, count, one, 0)
        down(slots)
        return carry

    lax.fori_loop(1, half_n, pair_step, 0)
    far = [slot(half_n)]

    def far_step(k, carry):
        gate_up(far, k)
        return carry

    lax.fori_loop(0, count, far_step, 0)
    down(far)
    for j in range(sent):
        for way in range(2):
            gather_copy(j, way).wait_send()

    bufs = (rbuf, lbuf)

    def sum_copy(j, way):
        return pltpu.make_async_remote_copy(
            src_ref=bufs[way].at[sent + j if j < 2 else j - 2],
            dst_ref=bufs[way].at[j],
            send_sem=send_sem.at[way, sent + j],
            recv_sem=recv_sem.at[way, sent + j],
            device_id=right if way == 0 else left,
            device_id_type=MESH,
        )

    for j in range(sent):
        for way in range(2):
            off = half_n - (j + 1) // 2
            owner = slot(n - off) if way == 0 else slot(off)
            c = (j + way) % 2
            own_part = acc[owner, part(c)]
            if j < 2:
                bufs[way][sent + j] = own_part
            else:
                sum_copy(j - 2, way).wait_recv()
                bufs[way][j - 2] = (bufs[way][j - 2].astype(jnp.float32) + own_part.astype(jnp.float32)).astype(jnp.bfloat16)
            sum_copy(j, way).start()
    for way in range(2):
        for j in (sent - 2, sent - 1):
            sum_copy(j, way).wait_recv()
    for c in range(2):
        total = hid_ref[part(c)] + acc[z, part(c)].astype(jnp.float32)
        for way in range(2):
            j = sent - 1 if (sent - 1 + way) % 2 == c else sent - 2
            total += bufs[way][j].astype(jnp.float32)
        out_ref[part(c)] = total.astype(jnp.bfloat16)
    for j in range(sent):
        for way in range(2):
            sum_copy(j, way).wait_send()


def mix_experts(normed, hidden, weight_table, inners, downs):
    rows, width = normed.shape
    n = lax.axis_size("z")
    pieces, count, depth, both = inners.shape
    ff = both // 2
    sent = n - 1
    vmem = pl.BlockSpec(memory_space=pltpu.VMEM)
    anywhere = pl.BlockSpec(memory_space=pl.ANY)
    return pl.pallas_call(
        functools.partial(moe_kernel, n),
        out_shape=jax.ShapeDtypeStruct((rows, width), jnp.bfloat16),
        in_specs=[vmem, vmem, vmem, anywhere, anywhere],
        out_specs=vmem,
        scratch_shapes=[
            pltpu.VMEM((n, rows, width), jnp.bfloat16),
            pltpu.VMEM((n, rows, width), jnp.bfloat16),
            pltpu.VMEM((count, 2 * rows, ff), jnp.bfloat16),
            pltpu.VMEM((count, pieces * depth, both), jnp.bfloat16),
            pltpu.VMEM((count, ff, pieces * depth), jnp.bfloat16),
            pltpu.VMEM((sent + 2, rows // 2, width), jnp.bfloat16),
            pltpu.VMEM((sent + 2, rows // 2, width), jnp.bfloat16),
            pltpu.SemaphoreType.DMA,
            pltpu.SemaphoreType.DMA((2, 2 * sent)),
            pltpu.SemaphoreType.DMA((2, 2 * sent)),
            pltpu.SemaphoreType.DMA((count, 2)),
        ],
        compiler_params=pltpu.CompilerParams(
            collective_id=0, has_side_effects=True, vmem_limit_bytes=66000000
        ),
        cost_estimate=pl.CostEstimate(
            flops=6 * n * rows * width * ff * count, bytes_accessed=40000000, transcendentals=0
        ),
    )(normed, hidden, weight_table, inners, downs)


def attend_items(query_items, key_items, value_items, segment_items):
    length, count_items, qk_width = query_items.shape
    block_rows = QUERY_BLOCK
    score_scale = qk_width ** (-0.5)
    key_positions = jnp.arange(length, dtype=jnp.int32)

    def one_block(block_index):
        first_row = block_index * block_rows
        query_block = lax.dynamic_slice_in_dim(query_items, first_row, block_rows, 0)
        scores = (
            jnp.einsum("qid,kid->iqk", query_block, key_items, preferred_element_type=jnp.float32)
            * score_scale
        )
        row_positions = first_row + jnp.arange(block_rows, dtype=jnp.int32)
        row_segments = lax.dynamic_slice_in_dim(segment_items, first_row, block_rows, 1)
        allowed = (row_positions[None, :, None] >= key_positions[None, None, :]) & (
            row_segments[:, :, None] == segment_items[:, None, :]
        )
        scores = jnp.where(allowed, scores, -jnp.inf)
        row_peak = jnp.max(scores, axis=2, keepdims=True)
        raised = jnp.exp(scores - row_peak)
        weights = (raised / jnp.sum(raised, axis=2, keepdims=True)).astype(jnp.bfloat16)
        return jnp.einsum(
            "iqk,kid->qid", weights, value_items, preferred_element_type=jnp.float32
        ).astype(jnp.bfloat16)

    blocks = lax.map(one_block, jnp.arange(length // block_rows, dtype=jnp.int32))
    return blocks.reshape(length, count_items, value_items.shape[2])


def column_weights(gate_matrix, up_matrix, down_matrix):
    parts = lax.axis_size(DP)
    depth = gate_matrix.shape[0] // parts
    first = lax.axis_index(DP) * depth
    gate_part = lax.dynamic_slice_in_dim(gate_matrix, first, depth, 0)
    up_part = lax.dynamic_slice_in_dim(up_matrix, first, depth, 0)
    main = gate_part.shape[1] // 128 * 128
    hidden_part = jnp.concatenate(
        [gate_part[:, :main], gate_part[:, main:], up_part[:, main:], up_part[:, :main]], axis=1
    )
    down_part = lax.dynamic_slice_in_dim(down_matrix, first, depth, 1)
    return [
        lax.all_gather(lax.all_gather(piece, "y"), DP) for piece in (hidden_part, down_part)
    ]


def column_table(routes, route_weights, expert_count):
    experts = jnp.arange(expert_count, dtype=jnp.int32)
    chosen = routes[:, :, None] == experts[None, None, :]
    table = jnp.sum(jnp.where(chosen, route_weights[:, :, None], 0.0), axis=1)
    table = lax.all_gather(table, "z")
    n = lax.axis_size("z")
    table = table.reshape(n, table.shape[1], expert_count // n, n)
    mine = jnp.arange(n, dtype=jnp.int32) == lax.axis_index("z")
    return jnp.sum(jnp.where(mine, table, 0.0), axis=3)


def body(
    queries,
    key_nope,
    key_rope,
    values,
    residual,
    segments,
    out_proj,
    norm_gain,
    expert_gate,
    expert_up,
    expert_down,
    routes,
    route_weights,
):
    half_rows, stream_count, query_width = queries.shape
    model_width = residual.shape[2]
    token_rows = half_rows * stream_count
    expert_count = lax.axis_size(EXPERT)
    item_count = stream_count * HEADS // expert_count
    inners, downs = column_weights(expert_gate[0], expert_up[0], expert_down[0])
    weight_table = column_table(routes[0, 0], route_weights[0, 0], expert_count)
    key_heads = jnp.concatenate(
        [
            key_nope.reshape(half_rows, stream_count, HEADS, NOPE),
            jnp.broadcast_to(key_rope[:, :, None, :], (half_rows, stream_count, HEADS, ROPE)),
        ],
        axis=3,
    )
    query_items = queries.reshape(half_rows, stream_count * HEADS, NOPE + ROPE)
    key_items = key_heads.reshape(half_rows, stream_count * HEADS, NOPE + ROPE)
    value_items = values.reshape(half_rows, stream_count * HEADS, V_DIM)
    query_all, key_all, value_all = side_by_side(
        (query_items, key_items, value_items), EXPERT, 1, 0, 2
    )
    item_ids = lax.axis_index(EXPERT) * item_count + jnp.arange(item_count, dtype=jnp.int32)
    stream_ids = item_ids // HEADS
    selector = (stream_ids[:, None] == jnp.arange(stream_count, dtype=jnp.int32)[None, :]).astype(
        jnp.int32
    )
    segment_items = jnp.sum(selector[:, :, None] * segments[None, :, :], axis=1)
    attended_items = attend_items(query_all, key_all, value_all, segment_items)
    attended_back = lax.all_to_all(
        attended_items, EXPERT, split_axis=0, concat_axis=1, tiled=True
    )
    attn_rows = attended_back.reshape(token_rows, HEADS * V_DIM)
    projected = jnp.dot(
        attn_rows,
        lax.all_gather(out_proj, DP + EXPERT, axis=0, tiled=True),
        preferred_element_type=jnp.float32,
    )
    hidden = residual.reshape(token_rows, model_width).astype(jnp.float32) + projected
    mean_square = jnp.mean(hidden * hidden, axis=1, keepdims=True)
    normed = (hidden * lax.rsqrt(mean_square + EPSILON) * norm_gain.astype(jnp.float32)).astype(
        jnp.bfloat16
    )
    layer_out = mix_experts(normed, hidden, weight_table, inners, downs)
    return layer_out.reshape(half_rows, stream_count, model_width)


def solution(mesh):
    split = Mesh(mesh.devices.reshape(4, 2, 4, 8), DP + EXPERT)
    rows = P(EXPERT, DP, None)
    weights = P(EXPERT, None, None)
    pairs = P(DP, EXPERT, None, None)
    return jax.shard_map(
        body,
        mesh=split,
        in_specs=(
            rows,
            rows,
            rows,
            rows,
            rows,
            P(DP, None),
            P(DP + EXPERT, None),
            P(),
            weights,
            weights,
            weights,
            pairs,
            pairs,
        ),
        out_specs=rows,
        check_vma=False,
    )
```

time: 492 us -> 511 us (1.039)
  Pallas kernels: 0 us -> 105 us
  waiting for transfers between devices: 180 us -> 285 us
  blocking collectives: 124 us -> 37.3 us
  local copies, waits for them, and re-layouts: 90.1 us -> 26.9 us
  matrix products: 38.3 us -> 16.7 us
  other arithmetic: 19.1 us -> 7.83 us
  starting transfers between devices: 22.7 us -> 15.7 us
    all_gather x1 -> x5, waiting for transfers between devices: 0.02 us -> 233 us  [the longest x2 159 us: column_weights(): lax.all_gather(lax.all_gather(piece, 'y'), DP)]
    all_to_all x2 -> x1, waiting for transfers between devices: 130 us -> 0.01 us  [body(): lax.all_to_all(attended_items, EXPERT, split_axis=0, concat_axis=1, tiled...]
    all_to_all x1 -> x0, blocking collectives: 124 us -> none  [body(): lax.all_to_all(outgoing, 'expert', split_axis=0, concat_axis=0, tiled=True)]
    pallas_call x0 -> x1, Pallas kernels: none -> 105 us  [mix_experts(): pl.pallas_call(functools.partial(moe_kernel, n), out_shape=jax.ShapeDtype...]
    all_gather x0 -> x1, blocking collectives: none -> 37.3 us  [column_table(): table = lax.all_gather(table, 'z')]
    gather x3 -> x0, local copies, waits for them, and re-layouts: 23.3 us -> none  [the longest x2 13.3 us: body(): slot_rows = normed[jnp.minimum(slot_source, pair_count - 1) // TOP]]
    reshape x3 -> x0, local copies, waits for them, and re-layouts: 21.8 us -> none  [the longest x1 7.29 us: body(): flat_rows = arrived.reshape(source_count * slot_count, width)]
    dot_general x4 -> x1, matrix products: 21.9 us -> 5.17 us  [body(): jnp.dot(attn_rows, lax.all_gather(out_proj, DP + EXPERT, axis=0, tiled=Tr...]
  transfers between devices with their start and end apart: 4 -> 7, of which waited for: 3 -> 5; matrix products, arithmetic and copies ran while one was open for 13% -> 9% of each run, Pallas kernels for 0% -> 0%
where the time goes in v1:
time: 511 us; the launch traced here: 510 us
  waiting for transfers between devices  285 us (56%)
  Pallas kernels  105 us (21%)
  blocking collectives  37.3 us (7%)
  local copies, waits for them, and re-layouts  26.9 us (5%)
  matrix products  16.7 us (3%)
  starting transfers between devices  15.7 us (3%)
  between operations  13.5 us (3%)
  other arithmetic  7.83 us (2%)
    all_gather x2, waiting for transfers between devices, column_weights(): lax.all_gather(lax.all_gather(piece, 'y'), DP)  159 us
    pallas_call x1, Pallas kernels, mix_experts(): pl.pallas_call(functools.partial(moe_kernel, n), out_shape=jax.ShapeDtype...  105 us
    all_gather x2, waiting for transfers between devices, column_weights(): lax.all_gather(piece, 'y')  73.9 us
    all_to_all x1, waiting for transfers between devices, side_by_side(): lax.all_to_all(both, axis, split_axis=split_dim, concat_axis=concat_dim,...  50.9 us
    all_gather x1, blocking collectives, column_table(): table = lax.all_gather(table, 'z')  37.3 us
  transfers between devices with their start and end apart: 7, of which 5 were waited for; matrix products, arithmetic and copies ran while one was open for 9% of the time, Pallas kernels for 0%

profile of v1, /device:TPU:2, one launch (start us, length us, event | category | flops | bytes accessed | tf_op | source)
XLA Modules:
  0.0 510.4 jit_solution(15161283140488874716)
XLA Ops:
  6.5 1.7 constant_dynamic-slice_fusion.1
  8.4 1.2 dynamic-slice_bitcast_fusion
  9.6 1.0 pad_maximum_fusion.1
  10.6 0.7 all-gather.10.cloned.1.call-update
  11.3 28.8 %all-gather.12.cloned.1.call-done = bf16[4,704,256]{2,1,0:T(8,128)(2,1)} async-done(((bf16[1,704,256]{2,1,0:T(8,128)(2,1)}), bf16[4,704,256]{2,1,0:T(8,128)(2,1)}) %all-gather.12.cloned.1.call-update) | async-done | bytes 1441808 | tf_op jit(solution)/shard_map/all_gather | solution.py:313
  40.2 45.2 %all-gather.14.cloned.1.call-done = bf16[1024,1408]{0,1:T(8,128)(2,1)} async-done(((bf16[256,1408]{0,1:T(8,128)(2,1)}), bf16[1024,1408]{0,1:T(8,128)(2,1)}) %all-gather.14.cloned.1.call-update) | async-done | bytes 2883600 | tf_op jit(solution)/shard_map/all_gather | solution.py:313
  85.3 4.6 copy.57
  90.0 1.2 reshape.112
  91.9 0.9 pad_maximum_fusion
  92.8 2.5 copy.50
  95.4 9.5 %all-to-all-start = ((bf16[64,32,512]{2,0,1:T(8,128)(2,1)}), bf16[64,32,512]{2,0,1:T(8,128)(2,1)S(1)}, u32[]{:S(2)}, u32[]{:S(2)}) async-start(bf16[64,32,512]{2,0,1:T(8,128)(2,1)} %copy.50), calls=%async_computation | async-start | bytes 4194304 | tf_op jit(solution)/shard_map/all_to_all | solution.py:28
  105.0 50.9 %all-to-all-done = bf16[64,32,512]{2,0,1:T(8,128)(2,1)S(1)} async-done(((bf16[64,32,512]{2,0,1:T(8,128)(2,1)}), bf16[64,32,512]{2,0,1:T(8,128)(2,1)S(1)}, u32[]{:S(2)}, u32[]{:S(2)}) %all-to-all-start) | async-done | bytes 2097184 | tf_op jit(solution)/shard_map/all_to_all | solution.py:28
  155.9 0.9 split.14
  156.8 1.4 fusion.15
  158.2 1.5 copy.51
  159.7 0.5 copy.52
  160.2 20.7 %while.11 = (s32[]{:T(128)}, bf16[4,512,1,128]{3,1,2,0:T(8,128)(2,1)}, s32[4]{0:T(128)S(1)}, s32[1,2048]{1,0:T(1,128)S(1)}, bf16[2048,1,192]{0,2,1:T(8,128)(2,1)...) while((s32[]{:T(128)}, ...), condition=%wide.region_4.5_spmd.clone, body=%wide.region_1.0_spmd.clone.sunk | while | flops 682688000 | bytes 16347855 | solution.py:297
  160.2 0.6 dynamic_slice.46
  161.5 1.3 fusion.23
  162.8 0.7 fusion.24
  163.9 1.5 fusion.25
  165.4 0.6 dynamic_slice.46
  166.7 1.3 fusion.23
  168.0 0.7 fusion.24
  169.1 1.5 fusion.25
  170.6 0.6 dynamic_slice.46
  171.8 1.3 fusion.23
  173.2 0.7 fusion.24
  174.2 1.5 fusion.25
  175.8 0.6 dynamic_slice.46
  177.0 1.3 fusion.23
  178.4 0.7 fusion.24
  179.4 1.5 fusion.25
  181.0 0.5 broadcast.52
  181.5 2.0 reduce.6
  183.4 0.9 reshape.127
  184.4 6.0 %all-to-all-start.1 = ((bf16[32,2,4096]{2,1,0:T(2,128)(2,1)}), bf16[32,2,4096]{2,1,0:T(2,128)(2,1)S(1)}, u32[]{:S(2)}, u32[]{:S(2)}) async-start(bf16[32,2,4096]{2,1,0:T(2,128)(2,1)} %reshape.127), calls=%async_computation.1 | async-start | bytes 1048576 | tf_op jit(solution)/shard_map/all_to_all | solution.py:370
  190.6 37.3 %all-gather = f32[1024,32]{0,1:T(8,128)S(1)} all-gather(f32[128,32]{0,1:T(8,128)S(1)} %select_reduce_fusion), channel_id=2, replica_groups=mesh['x'=4,'core'=2,'y'=4,'z'=8] {'z'}, dimensions={0}, use_global_device_ids=true | all-gather | bytes 147456 | tf_op jit(solution)/shard_map/all_gather | solution.py:321
  228.0 1.0 copy.56.wt_ref
  229.0 0.5 reshape.128
  229.7 0.3 copy.54
  230.3 5.2 %multiply_reduce_fusion = (f32[128]{0:T(128)S(1)}, f32[128,2048]{1,0:T(8,128)S(1)}) fusion(f32[128,2048]{1,0:T(8,128)S(1)} %reshape.118, bf16[128,2048]{1,0:T(8,128)(2,1)S(1)} %reshape.115, bf16[2048,2048]{1,0:T(8,128)(2,1)} %all-gather.10.cloned.1.call-done), kind=kOutput, calls=%fused_computation.21 | convolution fusion | flops 1074528128 | bytes 11010560 | tf_op jit(solution)/shard_map/dot_general | solution.py:374
  235.5 1.0 copy-done
  236.4 1.0 multiply_convert_fusion.x_ref
  237.4 42.9 %all-gather.18.cloned.1.call-done = bf16[32,704,256]{2,1,0:T(8,128)(2,1)} async-done(((bf16[4,704,256]{2,1,0:T(8,128)(2,1)}), bf16[32,704,256]{2,1,0:T(8,128)(2,1)}) %all-gather.18.cloned.1.call-update) | async-done | bytes 11534352 | tf_op jit(solution)/shard_map/all_gather | solution.py:313
  280.3 116.5 %all-gather.16.cloned.1.call-done = bf16[32,256,1408]{2,1,0:T(8,128)(2,1)} async-done(((bf16[4,256,1408]{2,1,0:T(8,128)(2,1)}), bf16[32,256,1408]{2,1,0:T(8,128)(2,1)}) %all-gather.16.cloned.1.call-update) | async-done | bytes 23068688 | tf_op jit(solution)/shard_map/all_gather | solution.py:313
  396.8 104.8 %shard_map.127 = bf16[128,2048]{1,0:T(8,128)(2,1)} custom-call(bf16[128,2048]{1,0:T(8,128)(2,1)} %multiply_convert_fusion.x_ref, f32[128,2048]{1,0:T(8,128)} %copy-done, f32[8,128,4]{2,1,0:T(8,128)} %copy.56.wt_ref, bf16[8,4,256,1408]{3,2,1,0:T(8,128)(2,1)} %bitcast.92, bf16[8,4,704,256]{3,2,1,0:T(8,128)(2,1)} %bitcast.93), custom_call_target="tpu_custom_call" | custom-call | flops 35433480192 | bytes 40000000 | tf_op jit(solution)/shard_map/pallas_call | solution.py:244
  501.7 2.2 reshape.117
  (65 shorter events, 3.1 us)
Async XLA Ops:
  6.5 33.5 %all-gather.12.cloned.1.call-start = ((), (), s32[]{:S(2)}) async-start(), calls=%async_computation.3 | async-start | bytes 1802240 | tf_op jit(solution)/shard_map/all_gather | solution.py:313
  8.3 77.0 %all-gather.14.cloned.1.call-start = ((), (), s32[]{:S(2)}) async-start(), calls=%async_computation.4 | async-start | bytes 3604480 | tf_op jit(solution)/shard_map/all_gather | solution.py:313
  10.5 219.7 %all-gather.10.cloned.1.call-start = ((), (), s32[]{:S(2)}) async-start(), calls=%async_computation.2 | async-start | bytes 8421376 | tf_op jit(solution)/shard_map/all_gather | solution.py:376
  11.3 269.0 %all-gather.18.cloned.1.call-start = ((), (), s32[]{:S(2)}) async-start(), calls=%async_computation.6 | async-start | bytes 12976128 | tf_op jit(solution)/shard_map/all_gather | solution.py:313
  40.1 49.9 %copy-start.1 = (bf16[64,2,3072]{2,1,0:T(2,128)(2,1)S(1)}, bf16[64,2,3072]{2,1,0:T(2,128)(2,1)}, u32[]{:S(2)}) copy-start(bf16[64,2,3072]{2,1,0:T(2,128)(2,1)} %param.15) | copy-start | bytes 2359300
  40.1 51.0 %copy-start.3 = (bf16[64,2,2048]{2,1,0:T(2,128)(2,1)S(1)}, bf16[64,2,2048]{2,1,0:T(2,128)(2,1)}, u32[]{:S(2)}) copy-start(bf16[64,2,2048]{2,1,0:T(2,128)(2,1)} %param.16) | copy-start | bytes 1572868
  40.1 356.7 %all-gather.16.cloned.1.call-start = ((), (), s32[]{:S(2)}) async-start(), calls=%async_computation.5 | async-start | bytes 25952256 | tf_op jit(solution)/shard_map/all_gather | solution.py:313
  89.9 1.6 copy-start.4
  89.9 1.9 copy-start.6
  92.8 12.1 %copy-start.7 = (s32[2,2048]{1,0:T(2,128)S(1)}, s32[2,2048]{1,0:T(2,128)}, u32[]{:S(2)}) copy-start(s32[2,2048]{1,0:T(2,128)} %param.20) | copy-start | bytes 49156
  95.4 60.6 %all-to-all-start = ((bf16[64,32,512]{2,0,1:T(8,128)(2,1)}), bf16[64,32,512]{2,0,1:T(8,128)(2,1)S(1)}, u32[]{:S(2)}, u32[]{:S(2)}) async-start(bf16[64,32,512]{2,0,1:T(8,128)(2,1)} %copy.50), calls=%async_computation | async-start | bytes 4194304 | tf_op jit(solution)/shard_map/all_to_all | solution.py:28
  160.2 30.2 %copy-start.2 = (bf16[64,2,2048]{2,1,0:T(2,128)(2,1)S(1)}, bf16[64,2,2048]{2,1,0:T(2,128)(2,1)}, u32[]{:S(2)}) copy-start(bf16[64,2,2048]{2,1,0:T(2,128)(2,1)} %param.19) | copy-start | bytes 1572868
  162.8 1.1 copy-start.5
  168.0 1.0 copy-start.5
  173.2 1.0 copy-start.5
  178.4 1.0 copy-start.5
  181.0 9.6 %copy-start.8 = (bf16[2048]{0:T(1024)(128)(2,1)S(1)}, bf16[2048]{0:T(1024)(128)(2,1)}, u32[]{:S(2)}) copy-start(bf16[2048]{0:T(1024)(128)(2,1)} %param.22) | copy-start | bytes 12292
  181.0 9.6 %copy-start.9 = (f32[1,1,128,6]{2,1,3,0:T(1,128)S(1)}, f32[1,1,128,6]{2,1,3,0:T(1,128)}, u32[]{:S(2)}) copy-start(f32[1,1,128,6]{2,1,3,0:T(1,128)} %param.27) | copy-start | bytes 9220
  181.0 9.6 %copy-start.10 = (s32[1,1,128,6]{2,1,3,0:T(1,128)S(1)}, s32[1,1,128,6]{2,1,3,0:T(1,128)}, u32[]{:S(2)}) copy-start(s32[1,1,128,6]{2,1,3,0:T(1,128)} %param.26) | copy-start | bytes 9220
  184.4 44.7 %all-to-all-start.1 = ((bf16[32,2,4096]{2,1,0:T(2,128)(2,1)}), bf16[32,2,4096]{2,1,0:T(2,128)(2,1)S(1)}, u32[]{:S(2)}, u32[]{:S(2)}) async-start(bf16[32,2,4096]{2,1,0:T(2,128)(2,1)} %reshape.127), calls=%async_computation.1 | async-start | bytes 1048576 | tf_op jit(solution)/shard_map/all_to_all | solution.py:370
  235.4 1.0 copy-start
Sparse Core Ops, SparseCore 0:
  9.1 30.8 all-gather.11
  41.9 43.4 all-gather.13
  89.1 126.6 all-gather.9
  217.4 62.8 all-gather.17
  282.0 114.7 all-gather.15

commit v2 on v1

--- a/solution.py
+++ b/solution.py
@@ -29,8 +29,9 @@
     return tuple(jnp.split(result, [sum(widths[:k]) for k in range(1, len(widths))], axis=along))
 
 
-def moe_kernel(axis_size, x_ref, hid_ref, wt_ref, wi_hbm, wd_hbm, out_ref,
-               xbuf, acc, act, wi, wd, rbuf, lbuf, start_sem, send_sem, recv_sem, wsem):
+def moe_kernel(axis_size, x_ref, hid_ref, wt_ref, own_g, own_u, own_d, *rest):
+    pieces = rest[:24]
+    (out_ref, xbuf, acc, act, weights, rbuf, lbuf, start_sem, send_sem, recv_sem, wsem) = rest[24:]
     n = axis_size
     half_n = n // 2
     z = lax.axis_index("z")
@@ -38,7 +39,8 @@
     left = {"z": lax.rem(z + n - 1, n)}
     rows = x_ref.shape[0]
     half = rows // 2
-    pieces, count, depth, ff = wi_hbm.shape[:3] + (wi_hbm.shape[3] // 2,)
+    count, _, ff, width = weights.shape
+    high, wide = pieces[0].shape[1:]
     sent = 2 * half_n - 1
 
     def slot(d):
@@ -47,14 +49,14 @@
     def part(c):
         return pl.ds(pl.multiple_of(c * half, half), half)
 
-    def fetch(k, carry):
-        for i in range(pieces):
-            span = pl.ds(i * depth, depth)
-            pltpu.make_async_copy(wi_hbm.at[i, k], wi.at[k, span], wsem.at[k, 0]).start()
-            pltpu.make_async_copy(wd_hbm.at[i, k], wd.at[k, :, span], wsem.at[k, 1]).start()
-        return carry
-
-    lax.fori_loop(0, count, fetch, 0)
+    for i, own in enumerate((own_g, own_u, own_d)):
+        pltpu.make_async_copy(own, weights.at[0, i], wsem.at[0]).start()
+    core = lax.axis_index("core")
+    for i, piece in enumerate(pieces):
+        k, quarter, half_of = 1 + i // 8, i % 8 // 2, i % 2
+        column = pl.multiple_of(lax.rem(core + half_of, 2) * wide, wide)
+        target = weights.at[k, :, pl.ds(quarter * high, high), pl.ds(column, wide)]
+        pltpu.make_async_copy(piece, target, wsem.at[k]).start()
 
     barrier = pltpu.get_barrier_semaphore()
     for neighbour in (left, right):
@@ -104,10 +106,7 @@
                 gather_copy(j + 2, way).start()
 
     lanes = lax.broadcasted_iota(jnp.int32, (1, wt_ref.shape[2]), 1)
-    main = ff // 128 * 128
-    rest = ff - main
-    cuts = [(a, min(a + 256, main)) for a in range(0, main, 256)]
-    width = xbuf.shape[2]
+    cuts = [(a, min(a + 256, ff)) for a in range(0, ff, 256)]
 
     def gate_up(slots, k):
         x = jnp.concatenate([xbuf[s] for s in slots], axis=0) if len(slots) > 1 else xbuf[slots[0]]
@@ -115,30 +114,24 @@
         scale = jnp.sum(jnp.where(lanes == k, wrow, 0.0), axis=1, keepdims=True)
         m = x.shape[0]
 
-        def product(lo, hi):
-            return jnp.dot(x, wi[k, :, lo:hi], preferred_element_type=jnp.float32)
-
-        def put(lo, hi, g, u):
+        def product(which, lo, hi):
+            return lax.dot_general(
+                x, weights[k, which, lo:hi], (((1,), (1,)), ((), ())), preferred_element_type=jnp.float32
+            )
+
+        for lo, hi in cuts:
+            g, u = product(0, lo, hi), product(1, lo, hi)
             a = g / (1.0 + jnp.exp(-g)) * u * scale
             act[k, 0:m, lo:hi] = a.astype(jnp.bfloat16)
 
-        start = main + 2 * rest
-        for lo, hi in cuts:
-            if hi == main and rest:
-                both = product(lo, start)
-                put(lo, hi, both[:, :hi - lo], product(start + lo, start + hi))
-                put(main, ff, both[:, hi - lo:hi - lo + rest], both[:, hi - lo + rest:])
-            else:
-                put(lo, hi, product(lo, hi), product(start + lo, start + hi))
-
     def down(slots):
         m = rows * len(slots)
 
         def columns(q, carry):
             span = pl.ds(pl.multiple_of(q * 512, min(512, width)), min(512, width))
-            y = jnp.dot(act[0, 0:m, :], wd[0, :, span], preferred_element_type=jnp.float32)
+            y = jnp.dot(act[0, 0:m, :], weights[0, 2, :, span], preferred_element_type=jnp.float32)
             for k in range(1, count):
-                y += jnp.dot(act[k, 0:m, :], wd[k, :, span], preferred_element_type=jnp.float32)
+                y += jnp.dot(act[k, 0:m, :], weights[k, 2, :, span], preferred_element_type=jnp.float32)
             y = y.astype(jnp.bfloat16)
             for i, s in enumerate(slots):
                 acc[s, :, span] = y[i * rows:(i + 1) * rows]
@@ -146,12 +139,12 @@
 
         lax.fori_loop(0, max(1, width // 512), columns, 0)
 
-    def fetched(k, which):
-        whole = (wi, wd)[which].at[k]
-        pltpu.make_async_copy(whole, whole, wsem.at[k, which]).wait()
+    def fetched(k):
+        whole = weights.at[k]
+        pltpu.make_async_copy(whole, whole, wsem.at[k]).wait()
 
     def own_step(k, carry):
-        fetched(k, 0)
+        fetched(k)
         gate_up([z], k)
 
         @pl.when(k == 1)
@@ -161,8 +154,6 @@
         return carry
 
     lax.fori_loop(0, count, own_step, 0)
-    for k in range(count):
-        fetched(k, 1)
     down([z])
 
     def pair_step(p, carry):
@@ -233,31 +224,31 @@
             sum_copy(j, way).wait_send()
 
 
-def mix_experts(normed, hidden, weight_table, inners, downs):
+def mix_experts(normed, hidden, weight_table, own_weights, other_weights):
     rows, width = normed.shape
     n = lax.axis_size("z")
-    pieces, count, depth, both = inners.shape
-    ff = both // 2
+    ff = own_weights[2].shape[0]
+    count = 1 + len(other_weights)
+    pieces = [half for source in other_weights for quarter in source for half in quarter]
     sent = n - 1
     vmem = pl.BlockSpec(memory_space=pltpu.VMEM)
     anywhere = pl.BlockSpec(memory_space=pl.ANY)
     return pl.pallas_call(
         functools.partial(moe_kernel, n),
         out_shape=jax.ShapeDtypeStruct((rows, width), jnp.bfloat16),
-        in_specs=[vmem, vmem, vmem, anywhere, anywhere],
+        in_specs=[vmem] * 3 + [anywhere] * (3 + len(pieces)),
         out_specs=vmem,
         scratch_shapes=[
             pltpu.VMEM((n, rows, width), jnp.bfloat16),
             pltpu.VMEM((n, rows, width), jnp.bfloat16),
             pltpu.VMEM((count, 2 * rows, ff), jnp.bfloat16),
-            pltpu.VMEM((count, pieces * depth, both), jnp.bfloat16),
-            pltpu.VMEM((count, ff, pieces * depth), jnp.bfloat16),
+            pltpu.VMEM((count, 3, ff, width), jnp.bfloat16),
             pltpu.VMEM((sent + 2, rows // 2, width), jnp.bfloat16),
             pltpu.VMEM((sent + 2, rows // 2, width), jnp.bfloat16),
             pltpu.SemaphoreType.DMA,
             pltpu.SemaphoreType.DMA((2, 2 * sent)),
             pltpu.SemaphoreType.DMA((2, 2 * sent)),
-            pltpu.SemaphoreType.DMA((count, 2)),
+            pltpu.SemaphoreType.DMA((count,)),
         ],
         compiler_params=pltpu.CompilerParams(
             collective_id=0, has_side_effects=True, vmem_limit_bytes=66000000
@@ -265,7 +256,7 @@
         cost_estimate=pl.CostEstimate(
             flops=6 * n * rows * width * ff * count, bytes_accessed=40000000, transcendentals=0
         ),
-    )(normed, hidden, weight_table, inners, downs)
+    )(normed, hidden, weight_table, *own_weights, *pieces)
 
 
 def attend_items(query_items, key_items, value_items, segment_items):
@@ -299,19 +290,30 @@
 
 
 def column_weights(gate_matrix, up_matrix, down_matrix):
-    parts = lax.axis_size(DP)
-    depth = gate_matrix.shape[0] // parts
-    first = lax.axis_index(DP) * depth
-    gate_part = lax.dynamic_slice_in_dim(gate_matrix, first, depth, 0)
-    up_part = lax.dynamic_slice_in_dim(up_matrix, first, depth, 0)
-    main = gate_part.shape[1] // 128 * 128
-    hidden_part = jnp.concatenate(
-        [gate_part[:, :main], gate_part[:, main:], up_part[:, main:], up_part[:, :main]], axis=1
-    )
-    down_part = lax.dynamic_slice_in_dim(down_matrix, first, depth, 1)
-    return [
-        lax.all_gather(lax.all_gather(piece, "y"), DP) for piece in (hidden_part, down_part)
-    ]
+    size_x, size_y = lax.axis_size("x"), lax.axis_size("y")
+    ff, width = down_matrix.shape
+    high, wide = ff // size_x, width // 2
+    mine, core = lax.axis_index("x"), lax.axis_index("core")
+
+    def piece(quarter):
+        first = (lax.rem(quarter, size_x) * high, core * wide)
+        return jnp.stack(
+            [lax.dynamic_slice(w, first, (high, wide)) for w in (gate_matrix, up_matrix, down_matrix)]
+        )
+
+    def shift(array, axis, by):
+        n = lax.axis_size(axis)
+        return lax.ppermute(array, axis, [(i, (i + by) % n) for i in range(n)])
+
+    one, two = piece(mine), piece(mine + 1)
+    left = [shift(one, "y", 1), shift(two, "y", 1)]
+    right = [shift(one, "y", -1), shift(two, "y", -1)]
+    far = [shift(left[0], "y", 1), shift(right[1], "y", -1)]
+    result = []
+    for source in (left, right, far):
+        quarters = source + [shift(source[1], "x", -1), shift(source[0], "x", 1)]
+        result.append([(quarter, shift(quarter, "core", 1)) for quarter in quarters])
+    return result
 
 
 def column_table(routes, route_weights, expert_count):
@@ -322,7 +324,11 @@
     n = lax.axis_size("z")
     table = table.reshape(n, table.shape[1], expert_count // n, n)
     mine = jnp.arange(n, dtype=jnp.int32) == lax.axis_index("z")
-    return jnp.sum(jnp.where(mine, table, 0.0), axis=3)
+    table = jnp.sum(jnp.where(mine, table, 0.0), axis=3)
+    count = expert_count // n
+    order = lax.rem(lax.axis_index("y") + jnp.array([0, count - 1, 1, 2], jnp.int32), count)
+    picks = order[:, None] == jnp.arange(count, dtype=jnp.int32)[None, :]
+    return jnp.sum(jnp.where(picks, table[:, :, None, :], 0.0), axis=3)
 
 
 def body(
@@ -345,7 +351,8 @@
     token_rows = half_rows * stream_count
     expert_count = lax.axis_size(EXPERT)
     item_count = stream_count * HEADS // expert_count
-    inners, downs = column_weights(expert_gate[0], expert_up[0], expert_down[0])
+    own_weights = (expert_gate[0].T, expert_up[0].T, expert_down[0])
+    other_weights = column_weights(*own_weights)
     weight_table = column_table(routes[0, 0], route_weights[0, 0], expert_count)
     key_heads = jnp.concatenate(
         [
@@ -381,7 +388,7 @@
     normed = (hidden * lax.rsqrt(mean_square + EPSILON) * norm_gain.astype(jnp.float32)).astype(
         jnp.bfloat16
     )
-    layer_out = mix_experts(normed, hidden, weight_table, inners, downs)
+    layer_out = mix_experts(normed, hidden, weight_table, own_weights, other_weights)
     return layer_out.reshape(half_rows, stream_count, model_width)
 
 

time: 511 us -> 361 us (0.71)
  waiting for transfers between devices: 285 us -> 117 us
  starting transfers between devices: 15.7 us -> 36.9 us
    all_gather x4 -> x0, waiting for transfers between devices: 233 us -> none  [the longest x2 159 us: column_weights(): lax.all_gather(lax.all_gather(piece, 'y'), DP)]
    ppermute x0 -> x24, waiting for transfers between devices: none -> 116 us  [shift(): return lax.ppermute(array, axis, [(i, (i + by) % n) for i in range(n)])]
    all_to_all x1, waiting for transfers between devices: 50.9 us -> 0.01 us  [side_by_side(): lax.all_to_all(both, axis, split_axis=split_dim, concat_axis=concat_dim,...]
    ppermute x0 -> x24, starting transfers between devices: none -> 18 us  [shift(): return lax.ppermute(array, axis, [(i, (i + by) % n) for i in range(n)])]
  transfers between devices with their start and end apart: 7 -> 27, of which waited for: 5 -> 8; matrix products, arithmetic and copies ran while one was open for 9% -> 12% of each run, Pallas kernels for 0% -> 0%
where the time goes in v2:
time: 361 us; the launch traced here: 358 us
  waiting for transfers between devices  117 us (32%)
  Pallas kernels  107 us (30%)
  starting transfers between devices  36.9 us (10%)
  blocking collectives  32.9 us (9%)
  local copies, waits for them, and re-layouts  24.2 us (7%)
  matrix products  16.3 us (5%)
  between operations  13.8 us (4%)
  other arithmetic  7.37 us (2%)
    ppermute x24, waiting for transfers between devices, shift(): return lax.ppermute(array, axis, [(i, (i + by) % n) for i in range(n)])  116 us
    pallas_call x1, Pallas kernels, mix_experts(): pl.pallas_call(functools.partial(moe_kernel, n), out_shape=jax.ShapeDtype...  107 us
    all_gather x1, blocking collectives, column_table(): table = lax.all_gather(table, 'z')  32.9 us
    ppermute x24, starting transfers between devices, shift(): return lax.ppermute(array, axis, [(i, (i + by) % n) for i in range(n)])  18 us
    all_to_all x1, starting transfers between devices, side_by_side(): lax.all_to_all(both, axis, split_axis=split_dim, concat_axis=concat_dim,...  11.5 us
    all_to_all x1, starting transfers between devices, body(): lax.all_to_all(attended_items, EXPERT, split_axis=0, concat_axis=1, tiled...  7.44 us
  transfers between devices with their start and end apart: 27, of which 8 were waited for; matrix products, arithmetic and copies ran while one was open for 12% of the time, Pallas kernels for 0%

profile of v2, /device:TPU:2, one launch (start us, length us, event | category | flops | bytes accessed | tf_op | source)
XLA Modules:
  0.0 358.0 jit_solution(13731966341199680332)
XLA Ops:
  7.3 1.4 concatenate.10
  8.6 1.4 reshape.127
  10.0 1.2 reshape.126
  11.3 0.9 pad_maximum_fusion
  12.2 2.5 copy.47
  14.7 11.5 %all-to-all-start = ((bf16[64,32,512]{2,0,1:T(8,128)(2,1)}), bf16[64,32,512]{2,0,1:T(8,128)(2,1)S(1)}, u32[]{:S(2)}, u32[]{:S(2)}) async-start(bf16[64,32,512]{2,0,1:T(8,128)(2,1)} %copy.47), calls=%async_computation | async-start | bytes 4194304 | tf_op jit(solution)/shard_map/all_to_all | solution.py:28
  26.2 1.2 constant_dynamic-slice_fusion.1
  27.4 1.4 dynamic-slice_bitcast_fusion
  29.0 3.1 collective-permute-start.8
  32.2 3.3 collective-permute-start.10
  35.5 40.6 %collective-permute-done.8.rest_8_ = bf16[3,176,1024]{2,1,0:T(8,128)(2,1)S(1)} collective-permute-done((bf16[3,176,1024]{2,1,0:T(8,128)(2,1)S(1)}, bf16[3,176,1024]{2,1,0:T(8,128)(2,1)S(1)}, u32[]{:S(2)}, u32[]{:S(2)}) %collective-permute-start.8) | collective-permute-done | bytes 1081376 | tf_op jit(solution)/shard_map/ppermute | solution.py:306
  76.2 1.5 collective-permute-start.14
  77.7 1.8 collective-permute-done.rest_0_
  80.0 19.0 %collective-permute-done.10.rest_10_ = bf16[3,176,1024]{2,1,0:T(8,128)(2,1)} collective-permute-done((bf16[3,176,1024]{2,1,0:T(8,128)(2,1)S(1)}, bf16[3,176,1024]{2,1,0:T(8,128)(2,1)}, u32[]{:S(2)}, u32[]{:S(2)}) %collective-permute-start.10) | collective-permute-done | bytes 1081376 | tf_op jit(solution)/shard_map/ppermute | solution.py:306
  99.0 1.5 collective-permute-start.6
  100.5 2.8 collective-permute-done.2.rest_2_
  103.3 1.1 collective-permute-start.18
  104.4 1.7 collective-permute-start.12
  106.1 29.1 %collective-permute-done.16.rest_16_ = bf16[3,176,1024]{2,1,0:T(8,128)(2,1)S(1)} collective-permute-done((bf16[3,176,1024]{2,1,0:T(8,128)(2,1)S(1)}, bf16[3,176,1024]{2,1,0:T(8,128)(2,1)S(1)}, u32[]{:S(2)}, u32[]{:S(2)}) %collective-permute-start.16) | collective-permute-done | bytes 1081376 | tf_op jit(solution)/shard_map/ppermute | solution.py:306
  135.3 2.0 collective-permute-start.4
  137.4 1.0 copy-done.15
  138.5 0.9 split.14
  139.4 1.5 fusion.16
  140.8 1.5 copy.49
  142.9 0.9 collective-permute-start.22
  144.2 21.0 %collective-permute-done.4.rest_4_ = bf16[3,176,1024]{2,1,0:T(8,128)(2,1)} collective-permute-done((bf16[3,176,1024]{2,1,0:T(8,128)(2,1)}, bf16[3,176,1024]{2,1,0:T(8,128)(2,1)}, u32[]{:S(2)}, u32[]{:S(2)}) %collective-permute-start.4) | collective-permute-done | bytes 1081376 | tf_op jit(solution)/shard_map/ppermute | solution.py:306
  165.8 19.8 %while.11 = (s32[]{:T(128)}, bf16[4,512,1,128]{3,1,2,0:T(8,128)(2,1)}, s32[4]{0:T(128)S(1)}, s32[1,2048]{1,0:T(1,128)S(1)}, bf16[2048,1,192]{0,2,1:T(8,128)(2,1)...) while((s32[]{:T(128)}, ...), condition=%wide.region_4.5_spmd.clone, body=%wide.region_1.0_spmd.clone.sunk | while | flops 682688000 | bytes 14250175 | solution.py:288
  167.2 1.3 fusion.24
  168.5 0.7 fusion.25
  169.2 1.5 fusion.26
  172.1 1.3 fusion.24
  174.2 1.5 fusion.26
  177.1 1.3 fusion.24
  178.4 0.7 fusion.25
  179.1 1.5 fusion.26
  182.0 1.3 fusion.24
  184.1 1.5 fusion.26
  186.2 2.0 reduce.6
  188.2 0.9 reshape.142
  189.1 7.4 %all-to-all-start.1 = ((bf16[32,2,4096]{2,1,0:T(2,128)(2,1)}), bf16[32,2,4096]{2,1,0:T(2,128)(2,1)S(1)}, u32[]{:S(2)}, u32[]{:S(2)}) async-start(bf16[32,2,4096]{2,1,0:T(2,128)(2,1)} %reshape.142), calls=%async_computation.1 | async-start | bytes 1048576 | tf_op jit(solution)/shard_map/all_to_all | solution.py:377
  196.7 32.9 %all-gather = f32[1024,32]{0,1:T(8,128)S(1)} all-gather(f32[128,32]{0,1:T(8,128)S(1)} %select_reduce_fusion), channel_id=2, replica_groups=mesh['x'=4,'core'=2,'y'=4,'z'=8] {'z'}, dimensions={0}, use_global_device_ids=true | all-gather | bytes 147456 | tf_op jit(solution)/shard_map/all_gather | solution.py:323
  229.9 1.1 copy.52.wt_ref
  233.8 4.8 %multiply_reduce_fusion = (f32[128]{0:T(128)S(1)}, f32[128,2048]{1,0:T(8,128)S(1)}) fusion(f32[128,2048]{1,0:T(8,128)S(1)} %reshape.136, bf16[128,2048]{1,0:T(8,128)(2,1)S(1)} %reshape.129, bf16[2048,2048]{1,0:T(8,128)(2,1)} %all-gather.3.cloned.1.call-done), kind=kOutput, calls=%fused_computation.23 | convolution fusion | flops 1074528128 | bytes 11010560 | tf_op jit(solution)/shard_map/dot_general | solution.py:381
  238.6 1.0 copy-done
  239.6 1.0 multiply_convert_fusion.x_ref
  240.5 1.3 collective-permute-done.21.rest_21_
  241.9 107.1 %shard_map.136 = bf16[128,2048]{1,0:T(8,128)(2,1)} custom-call(bf16[128,2048]{1,0:T(8,128)(2,1)} %multiply_convert_fusion.x_ref, f32[128,2048]{1,0:T(8,128)} %copy-done, f32[8,128,4]{2,1,0:T(8,128)} %copy.52.wt_ref, bf16[704,2048]{1,0:T(8,128)(2,1)} %bitcast.111, bf16[704,2048]{1,0:T(8,128)(2,1)} %bitcast.112, bf16[704,2048]{1,0:T(8,128)(2,1)} %bitcast.110, ...), custom_call_target="tpu_custom_call" | custom-call | flops 35433480192 | bytes 40000000 | tf_op jit(solution)/shard_map/pallas_call | solution.py:236
  349.0 2.2 reshape.135
  (108 shorter events, 11.1 us)
Async XLA Ops:
  6.5 3.5 copy-start.1
  6.5 4.7 %copy-start.4 = (bf16[64,2,64]{2,1,0:T(2,128)(2,1)S(1)}, bf16[64,2,64]{2,1,0:T(2,128)(2,1)}, u32[]{:S(2)}) copy-start(bf16[64,2,64]{2,1,0:T(2,128)(2,1)} %param.18) | copy-start | bytes 49156
  6.5 227.2 %all-gather.3.cloned.1.call-start = ((), (), s32[]{:S(2)}) async-start(), calls=%async_computation.2 | async-start | bytes 8421376 | tf_op jit(solution)/shard_map/all_gather | solution.py:383
  14.7 123.7 %all-to-all-start = ((bf16[64,32,512]{2,0,1:T(8,128)(2,1)}), bf16[64,32,512]{2,0,1:T(8,128)(2,1)S(1)}, u32[]{:S(2)}, u32[]{:S(2)}) async-start(bf16[64,32,512]{2,0,1:T(8,128)(2,1)} %copy.47), calls=%async_computation | async-start | bytes 4194304 | tf_op jit(solution)/shard_map/all_to_all | solution.py:28
  28.8 109.5 %copy-start.5 = (s32[2,2048]{1,0:T(2,128)S(1)}, s32[2,2048]{1,0:T(2,128)}, u32[]{:S(2)}) copy-start(s32[2,2048]{1,0:T(2,128)} %param.21) | copy-start | bytes 49156
  29.0 47.2 %collective-permute-start.8 = (bf16[3,176,1024]{2,1,0:T(8,128)(2,1)S(1)}, bf16[3,176,1024]{2,1,0:T(8,128)(2,1)S(1)}, u32[]{:S(2)}, u32[]{:S(2)}) collective-permute-start(bf16[3,176,1024]{2,1,0:T(8,128)(2,1)S(1)} %pad_maximum_fusion.1), channel_id=1, source_target_pairs={{0,24},{8,0},{16,8},{24,16},{1,25},{9,1},{17,9},{25,17},{2,26},{10... | collective-permute-start | bytes 3244040 | tf_op jit(solution)/shard_map/ppermute | solution.py:306
  32.1 47.4 %collective-permute-start = (bf16[3,176,1024]{2,1,0:T(8,128)(2,1)S(1)}, bf16[3,176,1024]{2,1,0:T(8,128)(2,1)S(1)}, u32[]{:S(2)}, u32[]{:S(2)}) collective-permute-start(bf16[3,176,1024]{2,1,0:T(8,128)(2,1)S(1)} %pad_maximum_fusion.1), channel_id=1, source_target_pairs={{0,8},{8,16},{16,24},{24,0},{1,9},{9,17},{17,25},{25,1},{2,10},{10... | collective-permute-start | bytes 3244040 | tf_op jit(solution)/shard_map/ppermute | solution.py:306
  32.2 66.8 %collective-permute-start.10 = (bf16[3,176,1024]{2,1,0:T(8,128)(2,1)S(1)}, bf16[3,176,1024]{2,1,0:T(8,128)(2,1)}, u32[]{:S(2)}, u32[]{:S(2)}) collective-permute-start(bf16[3,176,1024]{2,1,0:T(8,128)(2,1)S(1)} %pad_maximum_fusion.2), channel_id=1, source_target_pairs={{0,24},{8,0},{16,8},{24,16},{1,25},{9,1},{17,9},{25,17},{2,26},{10... | collective-permute-start | bytes 3244040 | tf_op jit(solution)/shard_map/ppermute | solution.py:306
  35.5 67.7 %collective-permute-start.2 = (bf16[3,176,1024]{2,1,0:T(8,128)(2,1)S(1)}, bf16[3,176,1024]{2,1,0:T(8,128)(2,1)}, u32[]{:S(2)}, u32[]{:S(2)}) collective-permute-start(bf16[3,176,1024]{2,1,0:T(8,128)(2,1)S(1)} %pad_maximum_fusion.2), channel_id=1, source_target_pairs={{0,8},{8,16},{16,24},{24,0},{1,9},{9,17},{17,25},{25,1},{2,10},{10... | collective-permute-start | bytes 3244040 | tf_op jit(solution)/shard_map/ppermute | solution.py:306
  76.2 27.1 %copy-start.9 = (bf16[3,176,1024]{2,1,0:T(8,128)(2,1)}, bf16[3,176,1024]{2,1,0:T(8,128)(2,1)S(1)}, u32[]{:S(2)}) copy-start(bf16[3,176,1024]{2,1,0:T(8,128)(2,1)S(1)} %collective-permute-done.8.rest_8_) | copy-start | bytes 3244036
  76.2 27.1 %collective-permute-start.14 = (bf16[3,176,1024]{2,1,0:T(8,128)(2,1)S(1)}, bf16[3,176,1024]{2,1,0:T(8,128)(2,1)S(1)}, u32[]{:S(2)}, u32[]{:S(2)}) collective-permute-start(bf16[3,176,1024]{2,1,0:T(8,128)(2,1)S(1)} %collective-permute-done.8.rest_8_), channel_id=1, source_target_pairs={{0,64},{64,128},{128,192},{192,0},{1,65},{65,129},{129,193},{193,1... | collective-permute-start | bytes 3244040 | tf_op jit(solution)/shard_map/ppermute | solution.py:306
  77.7 26.7 %collective-permute-start.9 = (bf16[3,176,1024]{2,1,0:T(8,128)(2,1)S(1)}, bf16[3,176,1024]{2,1,0:T(8,128)(2,1)S(1)}, u32[]{:S(2)}, u32[]{:S(2)}) collective-permute-start(bf16[3,176,1024]{2,1,0:T(8,128)(2,1)S(1)} %collective-permute-done.8.rest_8_), channel_id=1, source_target_pairs={{0,32},{32,0},{1,33},{33,1},{2,34},{34,2},{3,35},{35,3},{4,36},{36... | collective-permute-start | bytes 3244040 | tf_op jit(solution)/shard_map/ppermute | solution.py:306
  79.5 24.9 %copy-start.10 = (bf16[3,176,1024]{2,1,0:T(8,128)(2,1)}, bf16[3,176,1024]{2,1,0:T(8,128)(2,1)S(1)}, u32[]{:S(2)}) copy-start(bf16[3,176,1024]{2,1,0:T(8,128)(2,1)S(1)} %collective-permute-done.rest_0_) | copy-start | bytes 3244036
  79.5 55.6 %collective-permute-start.16 = (bf16[3,176,1024]{2,1,0:T(8,128)(2,1)S(1)}, bf16[3,176,1024]{2,1,0:T(8,128)(2,1)S(1)}, u32[]{:S(2)}, u32[]{:S(2)}) collective-permute-start(bf16[3,176,1024]{2,1,0:T(8,128)(2,1)S(1)} %collective-permute-done.rest_0_), channel_id=1, source_target_pairs={{0,8},{8,16},{16,24},{24,0},{1,9},{9,17},{17,25},{25,1},{2,10},{10... | collective-permute-start | bytes 3244040 | tf_op jit(solution)/shard_map/ppermute | solution.py:306
  99.0 36.3 %collective-permute-start.6 = (bf16[3,176,1024]{2,1,0:T(8,128)(2,1)S(1)}, bf16[3,176,1024]{2,1,0:T(8,128)(2,1)S(1)}, u32[]{:S(2)}, u32[]{:S(2)}) collective-permute-start(bf16[3,176,1024]{2,1,0:T(8,128)(2,1)S(1)} %collective-permute-done.rest_0_), channel_id=1, source_target_pairs={{0,64},{64,128},{128,192},{192,0},{1,65},{65,129},{129,193},{193,1... | collective-permute-start | bytes 3244040 | tf_op jit(solution)/shard_map/ppermute | solution.py:306
  103.3 34.1 %collective-permute-start.1 = (bf16[3,176,1024]{2,1,0:T(8,128)(2,1)S(1)}, bf16[3,176,1024]{2,1,0:T(8,128)(2,1)S(1)}, u32[]{:S(2)}, u32[]{:S(2)}) collective-permute-start(bf16[3,176,1024]{2,1,0:T(8,128)(2,1)S(1)} %collective-permute-done.rest_0_), channel_id=1, source_target_pairs={{0,32},{32,0},{1,33},{33,1},{2,34},{34,2},{3,35},{35,3},{4,36},{36... | collective-permute-start | bytes 3244040 | tf_op jit(solution)/shard_map/ppermute | solution.py:306
  103.3 34.1 %copy-start.11 = (bf16[3,176,1024]{2,1,0:T(8,128)(2,1)}, bf16[3,176,1024]{2,1,0:T(8,128)(2,1)S(1)}, u32[]{:S(2)}) copy-start(bf16[3,176,1024]{2,1,0:T(8,128)(2,1)S(1)} %collective-permute-done.14.rest_14_) | copy-start | bytes 3244036
  103.3 39.5 %collective-permute-start.18 = (bf16[3,176,1024]{2,1,0:T(8,128)(2,1)}, bf16[3,176,1024]{2,1,0:T(8,128)(2,1)}, u32[]{:S(2)}, u32[]{:S(2)}) collective-permute-start(bf16[3,176,1024]{2,1,0:T(8,128)(2,1)} %collective-permute-done.10.rest_10_), channel_id=1, source_target_pairs={{0,24},{8,0},{16,8},{24,16},{1,25},{9,1},{17,9},{25,17},{2,26},{10... | collective-permute-start | bytes 3244040 | tf_op jit(solution)/shard_map/ppermute | solution.py:306
  104.4 33.0 %copy-start.12 = (bf16[3,176,1024]{2,1,0:T(8,128)(2,1)}, bf16[3,176,1024]{2,1,0:T(8,128)(2,1)S(1)}, u32[]{:S(2)}) copy-start(bf16[3,176,1024]{2,1,0:T(8,128)(2,1)S(1)} %collective-permute-done.9.rest_9_) | copy-start | bytes 3244036
  104.4 39.3 %collective-permute-start.12 = (bf16[3,176,1024]{2,1,0:T(8,128)(2,1)}, bf16[3,176,1024]{2,1,0:T(8,128)(2,1)}, u32[]{:S(2)}, u32[]{:S(2)}) collective-permute-start(bf16[3,176,1024]{2,1,0:T(8,128)(2,1)} %collective-permute-done.10.rest_10_), channel_id=1, source_target_pairs={{0,192},{64,0},{128,64},{192,128},{1,193},{65,1},{129,65},{193,129... | collective-permute-start | bytes 3244040 | tf_op jit(solution)/shard_map/ppermute | solution.py:306
  135.2 2.2 copy-start.13
  135.2 8.6 %collective-permute-start.11 = (bf16[3,176,1024]{2,1,0:T(8,128)(2,1)}, bf16[3,176,1024]{2,1,0:T(8,128)(2,1)}, u32[]{:S(2)}, u32[]{:S(2)}) collective-permute-start(bf16[3,176,1024]{2,1,0:T(8,128)(2,1)} %collective-permute-done.10.rest_10_), channel_id=1, source_target_pairs={{0,32},{32,0},{1,33},{33,1},{2,34},{34,2},{3,35},{35,3},{4,36},{36... | collective-permute-start | bytes 3244040 | tf_op jit(solution)/shard_map/ppermute | solution.py:306
  135.3 2.0 copy-start.14
  135.3 29.9 %collective-permute-start.4 = (bf16[3,176,1024]{2,1,0:T(8,128)(2,1)}, bf16[3,176,1024]{2,1,0:T(8,128)(2,1)}, u32[]{:S(2)}, u32[]{:S(2)}) collective-permute-start(bf16[3,176,1024]{2,1,0:T(8,128)(2,1)} %collective-permute-done.2.rest_2_), channel_id=1, source_target_pairs={{0,192},{64,0},{128,64},{192,128},{1,193},{65,1},{129,65},{193,129... | collective-permute-start | bytes 3244040 | tf_op jit(solution)/shard_map/ppermute | solution.py:306
  137.4 1.0 copy-start.15
  138.4 26.9 %collective-permute-start.3 = (bf16[3,176,1024]{2,1,0:T(8,128)(2,1)}, bf16[3,176,1024]{2,1,0:T(8,128)(2,1)}, u32[]{:S(2)}, u32[]{:S(2)}) collective-permute-start(bf16[3,176,1024]{2,1,0:T(8,128)(2,1)} %collective-permute-done.2.rest_2_), channel_id=1, source_target_pairs={{0,32},{32,0},{1,33},{33,1},{2,34},{34,2},{3,35},{35,3},{4,36},{36... | collective-permute-start | bytes 3244040 | tf_op jit(solution)/shard_map/ppermute | solution.py:306
  140.8 25.0 %copy-start.3 = (bf16[2048,1,128]{2,0,1:T(8,128)(2,1)S(1)}, bf16[2048,1,128]{2,0,1:T(8,128)(2,1)}, u32[]{:S(2)}) copy-start(bf16[2048,1,128]{2,0,1:T(8,128)(2,1)} %split.14) | copy-start | bytes 1572868
  142.9 89.8 %collective-permute-start.22 = (bf16[3,176,1024]{2,1,0:T(8,128)(2,1)}, bf16[3,176,1024]{2,1,0:T(8,128)(2,1)}, u32[]{:S(2)}, u32[]{:S(2)}) collective-permute-start(bf16[3,176,1024]{2,1,0:T(8,128)(2,1)} %copy-done.13), channel_id=1, source_target_pairs={{0,64},{64,128},{128,192},{192,0},{1,65},{65,129},{129,193},{193,1... | collective-permute-start | bytes 3244040 | tf_op jit(solution)/shard_map/ppermute | solution.py:306
  143.7 89.4 %collective-permute-start.17 = (bf16[3,176,1024]{2,1,0:T(8,128)(2,1)}, bf16[3,176,1024]{2,1,0:T(8,128)(2,1)}, u32[]{:S(2)}, u32[]{:S(2)}) collective-permute-start(bf16[3,176,1024]{2,1,0:T(8,128)(2,1)} %copy-done.13), channel_id=1, source_target_pairs={{0,32},{32,0},{1,33},{33,1},{2,34},{34,2},{3,35},{35,3},{4,36},{36... | collective-permute-start | bytes 3244040 | tf_op jit(solution)/shard_map/ppermute | solution.py:306
  143.8 88.5 %collective-permute-start.15 = (bf16[3,176,1024]{2,1,0:T(8,128)(2,1)}, bf16[3,176,1024]{2,1,0:T(8,128)(2,1)}, u32[]{:S(2)}, u32[]{:S(2)}) collective-permute-start(bf16[3,176,1024]{2,1,0:T(8,128)(2,1)} %copy-done.11), channel_id=1, source_target_pairs={{0,32},{32,0},{1,33},{33,1},{2,34},{34,2},{3,35},{35,3},{4,36},{36... | collective-permute-start | bytes 3244040 | tf_op jit(solution)/shard_map/ppermute | solution.py:306
  165.3 68.0 %collective-permute-start.7 = (bf16[3,176,1024]{2,1,0:T(8,128)(2,1)}, bf16[3,176,1024]{2,1,0:T(8,128)(2,1)}, u32[]{:S(2)}, u32[]{:S(2)}) collective-permute-start(bf16[3,176,1024]{2,1,0:T(8,128)(2,1)} %copy-done.14), channel_id=1, source_target_pairs={{0,32},{32,0},{1,33},{33,1},{2,34},{34,2},{3,35},{35,3},{4,36},{36... | collective-permute-start | bytes 3244040 | tf_op jit(solution)/shard_map/ppermute | solution.py:306
  165.3 68.4 %collective-permute-start.20 = (bf16[3,176,1024]{2,1,0:T(8,128)(2,1)}, bf16[3,176,1024]{2,1,0:T(8,128)(2,1)}, u32[]{:S(2)}, u32[]{:S(2)}) collective-permute-start(bf16[3,176,1024]{2,1,0:T(8,128)(2,1)} %collective-permute-done.18.rest_18_), channel_id=1, source_target_pairs={{0,192},{64,0},{128,64},{192,128},{1,193},{65,1},{129,65},{193,129... | collective-permute-start | bytes 3244040 | tf_op jit(solution)/shard_map/ppermute | solution.py:306
  185.6 11.0 %copy-start.7 = (s32[1,1,128,6]{2,1,3,0:T(1,128)S(1)}, s32[1,1,128,6]{2,1,3,0:T(1,128)}, u32[]{:S(2)}) copy-start(s32[1,1,128,6]{2,1,3,0:T(1,128)} %param.27) | copy-start | bytes 9220
  185.6 11.0 %copy-start.8 = (f32[1,1,128,6]{2,1,3,0:T(1,128)S(1)}, f32[1,1,128,6]{2,1,3,0:T(1,128)}, u32[]{:S(2)}) copy-start(f32[1,1,128,6]{2,1,3,0:T(1,128)} %param.28) | copy-start | bytes 9220
  185.6 11.0 %copy-start.6 = (bf16[2048]{0:T(1024)(128)(2,1)S(1)}, bf16[2048]{0:T(1024)(128)(2,1)}, u32[]{:S(2)}) copy-start(bf16[2048]{0:T(1024)(128)(2,1)} %param.23) | copy-start | bytes 12292
  185.6 44.1 %copy-start.16 = (s32[4]{0:T(128)S(1)}, s32[4]{0:T(128)}, u32[]{:S(2)}) copy-start(s32[4]{0:T(128)} %constant.99.clone) | copy-start | bytes 52
  185.6 45.3 %copy-start.2 = (bf16[64,2,2048]{2,1,0:T(2,128)(2,1)S(1)}, bf16[64,2,2048]{2,1,0:T(2,128)(2,1)}, u32[]{:S(2)}) copy-start(bf16[64,2,2048]{2,1,0:T(2,128)(2,1)} %param.20) | copy-start | bytes 1572868
  189.1 42.0 %all-to-all-start.1 = ((bf16[32,2,4096]{2,1,0:T(2,128)(2,1)}), bf16[32,2,4096]{2,1,0:T(2,128)(2,1)S(1)}, u32[]{:S(2)}, u32[]{:S(2)}) async-start(bf16[32,2,4096]{2,1,0:T(2,128)(2,1)} %reshape.142), calls=%async_computation.1 | async-start | bytes 1048576 | tf_op jit(solution)/shard_map/all_to_all | solution.py:377
  232.3 8.2 %collective-permute-start.19 = (bf16[3,176,1024]{2,1,0:T(8,128)(2,1)}, bf16[3,176,1024]{2,1,0:T(8,128)(2,1)}, u32[]{:S(2)}, u32[]{:S(2)}) collective-permute-start(bf16[3,176,1024]{2,1,0:T(8,128)(2,1)} %collective-permute-done.18.rest_18_), channel_id=1, source_target_pairs={{0,32},{32,0},{1,33},{33,1},{2,34},{34,2},{3,35},{35,3},{4,36},{36... | collective-permute-start | bytes 3244040 | tf_op jit(solution)/shard_map/ppermute | solution.py:306
  232.7 7.9 %collective-permute-start.13 = (bf16[3,176,1024]{2,1,0:T(8,128)(2,1)}, bf16[3,176,1024]{2,1,0:T(8,128)(2,1)}, u32[]{:S(2)}, u32[]{:S(2)}) collective-permute-start(bf16[3,176,1024]{2,1,0:T(8,128)(2,1)} %collective-permute-done.12.rest_12_), channel_id=1, source_target_pairs={{0,32},{32,0},{1,33},{33,1},{2,34},{34,2},{3,35},{35,3},{4,36},{36... | collective-permute-start | bytes 3244040 | tf_op jit(solution)/shard_map/ppermute | solution.py:306
  233.2 7.4 %collective-permute-start.5 = (bf16[3,176,1024]{2,1,0:T(8,128)(2,1)}, bf16[3,176,1024]{2,1,0:T(8,128)(2,1)}, u32[]{:S(2)}, u32[]{:S(2)}) collective-permute-start(bf16[3,176,1024]{2,1,0:T(8,128)(2,1)} %collective-permute-done.4.rest_4_), channel_id=1, source_target_pairs={{0,32},{32,0},{1,33},{33,1},{2,34},{34,2},{3,35},{35,3},{4,36},{36... | collective-permute-start | bytes 3244040 | tf_op jit(solution)/shard_map/ppermute | solution.py:306
  233.3 7.3 %collective-permute-start.23 = (bf16[3,176,1024]{2,1,0:T(8,128)(2,1)}, bf16[3,176,1024]{2,1,0:T(8,128)(2,1)}, u32[]{:S(2)}, u32[]{:S(2)}) collective-permute-start(bf16[3,176,1024]{2,1,0:T(8,128)(2,1)} %collective-permute-done.22.rest_22_), channel_id=1, source_target_pairs={{0,32},{32,0},{1,33},{33,1},{2,34},{34,2},{3,35},{35,3},{4,36},{36... | collective-permute-start | bytes 3244040 | tf_op jit(solution)/shard_map/ppermute | solution.py:306
  233.7 8.2 %collective-permute-start.21 = (bf16[3,176,1024]{2,1,0:T(8,128)(2,1)}, bf16[3,176,1024]{2,1,0:T(8,128)(2,1)}, u32[]{:S(2)}, u32[]{:S(2)}) collective-permute-start(bf16[3,176,1024]{2,1,0:T(8,128)(2,1)} %collective-permute-done.20.rest_20_), channel_id=1, source_target_pairs={{0,32},{32,0},{1,33},{33,1},{2,34},{34,2},{3,35},{35,3},{4,36},{36... | collective-permute-start | bytes 3244040 | tf_op jit(solution)/shard_map/ppermute | solution.py:306
  238.5 1.0 copy-start
Sparse Core Ops, SparseCore 0:
  11.0 129.8 all-gather.2

commit v3 on v2

--- a/solution.py
+++ b/solution.py
@@ -22,25 +22,286 @@
 QUERY_BLOCK = 512
 
 
-def side_by_side(arrays, axis, split_dim, concat_dim, along):
-    widths = [a.shape[along] for a in arrays]
-    both = jnp.concatenate(arrays, axis=along)
-    result = lax.all_to_all(both, axis, split_axis=split_dim, concat_axis=concat_dim, tiled=True)
-    return tuple(jnp.split(result, [sum(widths[:k]) for k in range(1, len(widths))], axis=along))
-
-
-def moe_kernel(axis_size, x_ref, hid_ref, wt_ref, own_g, own_u, own_d, *rest):
-    pieces = rest[:24]
-    (out_ref, xbuf, acc, act, weights, rbuf, lbuf, start_sem, send_sem, recv_sem, wsem) = rest[24:]
+def front_kernel(qkv, bound, table, own_g, own_u, own_d, attn_ref, tab_ref, others,
+                 rows_buf, qbuf, kbuf, att, local_sem, a2a_sem, att_sem, tab_sem,
+                 ysend, yrecv, fsend, frecv, xsend, xrecv, csend, crecv):
+    size_x, size_y, size_z = lax.axis_size("x"), lax.axis_size("y"), lax.axis_size("z")
+    peers = size_y * size_z
+    x, core = lax.axis_index("x"), lax.axis_index("core")
+    y, z = lax.axis_index("y"), lax.axis_index("z")
+    me = y * size_z + z
+    up_y, down_y = {"y": lax.rem(y + 1, size_y)}, {"y": lax.rem(y + size_y - 1, size_y)}
+    up_x, down_x = {"x": lax.rem(x + 1, size_x)}, {"x": lax.rem(x + size_x - 1, size_x)}
+    other_core = {"core": 1 - core}
+    block = qkv.shape[1]
+    heads = attn_ref.shape[1] // V_DIM
+    ff, width = own_d.shape
+    high, wide = ff // size_x, width // 4
+
+    def peer(e):
+        return {"y": lax.div(e, size_z), "z": lax.rem(e, size_z)}
+
+    def remote(src, dst, send, recv, device):
+        return pltpu.make_async_remote_copy(
+            src_ref=src, dst_ref=dst, send_sem=send, recv_sem=recv, device_id=device, device_id_type=MESH
+        )
+
+    barrier = pltpu.get_barrier_semaphore()
+
+    def greet(d, carry):
+        pl.semaphore_signal(barrier, inc=1, device_id=peer(lax.rem(me + d, peers)), device_id_type=MESH)
+        return carry
+
+    lax.fori_loop(1, peers, greet, 0)
+    for device in (up_x, down_x, other_core):
+        pl.semaphore_signal(barrier, inc=1, device_id=device, device_id_type=MESH)
+    pl.semaphore_wait(barrier, peers + 2)
+
+    def rows_of(e):
+        return pl.ds(pl.multiple_of(e * block, block), block)
+
+    def send_rows(d, carry):
+        e = lax.rem(me + d, peers)
+        remote(qkv.at[e], rows_buf.at[rows_of(me)], a2a_sem.at[0], a2a_sem.at[1], peer(e)).start()
+        return carry
+
+    lax.fori_loop(1, peers, send_rows, 0)
+    own_rows = pltpu.make_async_copy(qkv.at[me], rows_buf.at[rows_of(me)], local_sem.at[0])
+    own_rows.start()
+
+    def columns(u):
+        return pl.ds(pl.multiple_of((core * 2 + u) * wide, wide), wide)
+
+    def region(s, q, u):
+        return others.at[s, :, pl.ds(q * high, high), columns(u)]
+
+    def y_index(s, q, u):
+        return (s * 2 + q) * 2 + u
+
+    def y_start(s, q, u):
+        n = y_index(s, q, u)
+        quarter = pl.ds(pl.multiple_of(lax.rem(x + q, size_x) * high, high), high)
+        for m, own in enumerate((own_g, own_u, own_d)):
+            remote(
+                own.at[quarter, columns(u)],
+                others.at[s, m, pl.ds(q * high, high), columns(u)],
+                ysend.at[n],
+                yrecv.at[n],
+                up_y if s == 0 else down_y,
+            ).start()
+
+    def y_copy(s, q, u):
+        n = y_index(s, q, u)
+        return remote(region(s, q, u), region(s, q, u), ysend.at[n], yrecv.at[n], up_y)
+
+    def f_copy(q, u):
+        source, device = (0, up_y) if q == 0 else (1, down_y)
+        n = q * 2 + u
+        return remote(region(source, q, u), region(2, q, u), fsend.at[n], frecv.at[n], device)
+
+    def x_copy(s, q, u):
+        device, slot = (up_x, 3) if q == 0 else (down_x, 2)
+        n = (s * 2 + q) * 2 + u
+        return remote(region(s, q, u), region(s, slot, u), xsend.at[n], xrecv.at[n], device)
+
+    def c_copy(s, q, u):
+        n = (s * 4 + q) * 2 + u
+        return remote(region(s, q, u), region(s, q, u), csend.at[n], crecv.at[n], other_core)
+
+    for first in (True, False):
+        for u in range(2):
+            for s in range(2):
+                y_start(s, s if first else 1 - s, u)
+
+    def tab_copy(d):
+        to = lax.rem(z + d, size_z)
+        return remote(table.at[to], tab_ref.at[z], tab_sem.at[0], tab_sem.at[1], {"z": to})
+
+    for d in range(1, size_z):
+        tab_copy(d).start()
+    own_table = pltpu.make_async_copy(table.at[z], tab_ref.at[z], local_sem.at[1])
+    own_table.start()
+
+    def arrived(s, q, u):
+        x_copy(s, q, u).start()
+        c_copy(s, q, u).start()
+
+    for u in range(2):
+        for s in range(2):
+            y_copy(s, s, u).wait_recv()
+            f_copy(s, u).start()
+            arrived(s, s, u)
+
+    own_rows.wait()
+    most = rows_buf.at[pl.ds(0, (peers - 1) * block)]
+    remote(most, most, a2a_sem.at[0], a2a_sem.at[1], up_y).wait_recv()
+
+    length = rows_buf.shape[0]
+    lane = lax.broadcasted_iota(jnp.int32, (1, 128), 1)
+    swap = (
+        lax.broadcasted_iota(jnp.int32, (128, 128), 0) == lax.broadcasted_iota(jnp.int32, (128, 128), 1) + ROPE
+    ).astype(jnp.bfloat16)
+
+    step = min(512, length)
+    strip = min(256, step)
+
+    def arrange(i, carry):
+        span = pl.ds(pl.multiple_of(i * step, step), step)
+        rope = rows_buf[span, 384:512]
+        qbuf[span, 0:128] = rows_buf[span, 0:128]
+        qbuf[span, 128:256] = jnp.where(lane < ROPE, rope, jnp.zeros_like(rope))
+        kbuf[span, 0:128] = rows_buf[span, 128:256]
+        kbuf[span, 128:256] = jnp.dot(rope, swap, preferred_element_type=jnp.float32).astype(jnp.bfloat16)
+        return carry
+
+    lax.fori_loop(0, length // step, arrange, 0)
+    border = bound[0]
+    scale = (NOPE + ROPE) ** (-0.5)
+    stream, head = lax.div(me, heads), lax.rem(me, heads)
+    target = (
+        pl.ds(pl.multiple_of(stream * block, block), block),
+        pl.ds(pl.multiple_of(head * V_DIM, V_DIM), V_DIM),
+    )
+
+    def back_copy(e):
+        return remote(att.at[rows_of(e)], attn_ref.at[target[0], target[1]], att_sem.at[0], att_sem.at[1], peer(e))
+
+    def local_back():
+        return pltpu.make_async_copy(att.at[rows_of(me)], attn_ref.at[target[0], target[1]], local_sem.at[2])
+
+    def attend(i):
+        limit = (i + 1) * step
+
+        def one(j, carry):
+            first = i * step + j * strip
+            span = pl.ds(pl.multiple_of(first, strip), strip)
+            scores = lax.dot_general(
+                qbuf[span, :], kbuf[0:limit, :], (((1,), (1,)), ((), ())), preferred_element_type=jnp.float32
+            ) * scale
+            row = first + lax.broadcasted_iota(jnp.int32, (strip, 1), 0)
+            column = lax.broadcasted_iota(jnp.int32, (1, limit), 1)
+            lowest = jnp.where(row >= border, border, 0)
+            scores = jnp.where((column <= row) & (column >= lowest), scores, -jnp.inf)
+            raised = jnp.exp(scores - jnp.max(scores, axis=1, keepdims=True))
+            total = jnp.sum(raised, axis=1, keepdims=True)
+            mixed = jnp.dot(
+                raised.astype(jnp.bfloat16), rows_buf[0:limit, 256:384], preferred_element_type=jnp.float32
+            )
+            att[span, :] = (mixed / total).astype(jnp.bfloat16)
+            for t in range(strip // block):
+                e = lax.div(first, block) + t
+
+                @pl.when(e != me)
+                def _():
+                    back_copy(e).start()
+
+                @pl.when(e == me)
+                def _():
+                    local_back().start()
+
+            return carry
+
+        lax.fori_loop(0, step // strip, one, 0)
+
+    count = length // step
+    for i in range(count):
+        attend(i)
+        if i == count // 2 - 1:
+            for u in range(2):
+                for s in range(2):
+                    y_copy(s, 1 - s, u).wait_recv()
+                    arrived(s, 1 - s, u)
+
+    def crossed(s, q, u):
+        x_copy(s, q, u).wait_recv()
+        c_copy(s, 3 if q == 0 else 2, u).start()
+
+    for u in range(2):
+        for s in range(2):
+            crossed(s, s, u)
+    for u in range(2):
+        for q in range(2):
+            f_copy(q, u).wait_recv()
+            arrived(2, q, u)
+    for u in range(2):
+        for s in range(2):
+            crossed(s, 1 - s, u)
+    for u in range(2):
+        for q in range(2):
+            crossed(2, q, u)
+
+    for s in range(3):
+        for q in range(4):
+            for u in range(2):
+                c_copy(s, q, u).wait()
+    for u in range(2):
+        for q in range(2):
+            for s in range(2):
+                y_copy(s, q, u).wait_send()
+            f_copy(q, u).wait_send()
+            for s in range(3):
+                x_copy(s, q, u).wait_send()
+    remote(most, most, a2a_sem.at[0], a2a_sem.at[1], up_y).wait_send()
+    local_back().wait()
+    back = att.at[pl.ds(0, (peers - 1) * block)]
+    remote(back, back, att_sem.at[0], att_sem.at[1], up_y).wait()
+    own_table.wait()
+    tables = tab_ref.at[pl.ds(0, size_z - 1)]
+    remote(tables, tables, tab_sem.at[0], tab_sem.at[1], up_y).wait()
+
+
+def attend_and_gather(qkv, bound, table, own_weights):
+    peers, block, packed = qkv.shape
+    ff, width = own_weights[2].shape
+    heads = width // V_DIM
+    length = peers * block
+    vmem = pl.BlockSpec(memory_space=pltpu.VMEM)
+    anywhere = pl.BlockSpec(memory_space=pl.ANY)
+    dma = pltpu.SemaphoreType.DMA
+    return pl.pallas_call(
+        front_kernel,
+        out_shape=(
+            jax.ShapeDtypeStruct((peers // heads * block, width), jnp.bfloat16),
+            jax.ShapeDtypeStruct(table.shape, jnp.float32),
+            jax.ShapeDtypeStruct((3, 3, ff, width), jnp.bfloat16),
+        ),
+        in_specs=[anywhere, pl.BlockSpec(memory_space=pltpu.SMEM), vmem] + [anywhere] * 3,
+        out_specs=(vmem, vmem, anywhere),
+        scratch_shapes=[
+            pltpu.VMEM((length, packed), jnp.bfloat16),
+            pltpu.VMEM((length, 256), jnp.bfloat16),
+            pltpu.VMEM((length, 256), jnp.bfloat16),
+            pltpu.VMEM((length, V_DIM), jnp.bfloat16),
+            dma((3,)),
+            dma((2,)),
+            dma((2,)),
+            dma((2,)),
+            dma((8,)),
+            dma((8,)),
+            dma((4,)),
+            dma((4,)),
+            dma((12,)),
+            dma((12,)),
+            dma((24,)),
+            dma((24,)),
+        ],
+        compiler_params=pltpu.CompilerParams(
+            collective_id=1, has_side_effects=True, vmem_limit_bytes=50000000
+        ),
+        cost_estimate=pl.CostEstimate(flops=100000000000, bytes_accessed=40000000, transcendentals=0),
+    )(qkv, bound, table, *own_weights)
+
+
+def moe_kernel(axis_size, x_ref, hid_ref, wt_ref, own_g, own_u, own_d, others,
+               out_ref, xbuf, acc, act, weights, rbuf, lbuf, start_sem, send_sem, recv_sem, wsem):
     n = axis_size
     half_n = n // 2
-    z = lax.axis_index("z")
+    y, z = lax.axis_index("y"), lax.axis_index("z")
     right = {"z": lax.rem(z + 1, n)}
     left = {"z": lax.rem(z + n - 1, n)}
     rows = x_ref.shape[0]
     half = rows // 2
     count, _, ff, width = weights.shape
-    high, wide = pieces[0].shape[1:]
     sent = 2 * half_n - 1
 
     def slot(d):
@@ -51,12 +312,8 @@
 
     for i, own in enumerate((own_g, own_u, own_d)):
         pltpu.make_async_copy(own, weights.at[0, i], wsem.at[0]).start()
-    core = lax.axis_index("core")
-    for i, piece in enumerate(pieces):
-        k, quarter, half_of = 1 + i // 8, i % 8 // 2, i % 2
-        column = pl.multiple_of(lax.rem(core + half_of, 2) * wide, wide)
-        target = weights.at[k, :, pl.ds(quarter * high, high), pl.ds(column, wide)]
-        pltpu.make_async_copy(piece, target, wsem.at[k]).start()
+    for k in range(1, count):
+        pltpu.make_async_copy(others.at[k - 1], weights.at[k], wsem.at[k]).start()
 
     barrier = pltpu.get_barrier_semaphore()
     for neighbour in (left, right):
@@ -111,7 +368,8 @@
     def gate_up(slots, k):
         x = jnp.concatenate([xbuf[s] for s in slots], axis=0) if len(slots) > 1 else xbuf[slots[0]]
         wrow = jnp.concatenate([wt_ref[s] for s in slots], axis=0) if len(slots) > 1 else wt_ref[slots[0]]
-        scale = jnp.sum(jnp.where(lanes == k, wrow, 0.0), axis=1, keepdims=True)
+        offset = jnp.where(k == 0, 0, jnp.where(k == 1, count - 1, k - 1))
+        scale = jnp.sum(jnp.where(lanes == lax.rem(y + offset, count), wrow, 0.0), axis=1, keepdims=True)
         m = x.shape[0]
 
         def product(which, lo, hi):
@@ -228,15 +486,14 @@
     rows, width = normed.shape
     n = lax.axis_size("z")
     ff = own_weights[2].shape[0]
-    count = 1 + len(other_weights)
-    pieces = [half for source in other_weights for quarter in source for half in quarter]
+    count = 1 + other_weights.shape[0]
     sent = n - 1
     vmem = pl.BlockSpec(memory_space=pltpu.VMEM)
     anywhere = pl.BlockSpec(memory_space=pl.ANY)
     return pl.pallas_call(
         functools.partial(moe_kernel, n),
         out_shape=jax.ShapeDtypeStruct((rows, width), jnp.bfloat16),
-        in_specs=[vmem] * 3 + [anywhere] * (3 + len(pieces)),
+        in_specs=[vmem] * 3 + [anywhere] * 4,
         out_specs=vmem,
         scratch_shapes=[
             pltpu.VMEM((n, rows, width), jnp.bfloat16),
@@ -256,79 +513,14 @@
         cost_estimate=pl.CostEstimate(
             flops=6 * n * rows * width * ff * count, bytes_accessed=40000000, transcendentals=0
         ),
-    )(normed, hidden, weight_table, *own_weights, *pieces)
-
-
-def attend_items(query_items, key_items, value_items, segment_items):
-    length, count_items, qk_width = query_items.shape
-    block_rows = QUERY_BLOCK
-    score_scale = qk_width ** (-0.5)
-    key_positions = jnp.arange(length, dtype=jnp.int32)
-
-    def one_block(block_index):
-        first_row = block_index * block_rows
-        query_block = lax.dynamic_slice_in_dim(query_items, first_row, block_rows, 0)
-        scores = (
-            jnp.einsum("qid,kid->iqk", query_block, key_items, preferred_element_type=jnp.float32)
-            * score_scale
-        )
-        row_positions = first_row + jnp.arange(block_rows, dtype=jnp.int32)
-        row_segments = lax.dynamic_slice_in_dim(segment_items, first_row, block_rows, 1)
-        allowed = (row_positions[None, :, None] >= key_positions[None, None, :]) & (
-            row_segments[:, :, None] == segment_items[:, None, :]
-        )
-        scores = jnp.where(allowed, scores, -jnp.inf)
-        row_peak = jnp.max(scores, axis=2, keepdims=True)
-        raised = jnp.exp(scores - row_peak)
-        weights = (raised / jnp.sum(raised, axis=2, keepdims=True)).astype(jnp.bfloat16)
-        return jnp.einsum(
-            "iqk,kid->qid", weights, value_items, preferred_element_type=jnp.float32
-        ).astype(jnp.bfloat16)
-
-    blocks = lax.map(one_block, jnp.arange(length // block_rows, dtype=jnp.int32))
-    return blocks.reshape(length, count_items, value_items.shape[2])
-
-
-def column_weights(gate_matrix, up_matrix, down_matrix):
-    size_x, size_y = lax.axis_size("x"), lax.axis_size("y")
-    ff, width = down_matrix.shape
-    high, wide = ff // size_x, width // 2
-    mine, core = lax.axis_index("x"), lax.axis_index("core")
-
-    def piece(quarter):
-        first = (lax.rem(quarter, size_x) * high, core * wide)
-        return jnp.stack(
-            [lax.dynamic_slice(w, first, (high, wide)) for w in (gate_matrix, up_matrix, down_matrix)]
-        )
-
-    def shift(array, axis, by):
-        n = lax.axis_size(axis)
-        return lax.ppermute(array, axis, [(i, (i + by) % n) for i in range(n)])
-
-    one, two = piece(mine), piece(mine + 1)
-    left = [shift(one, "y", 1), shift(two, "y", 1)]
-    right = [shift(one, "y", -1), shift(two, "y", -1)]
-    far = [shift(left[0], "y", 1), shift(right[1], "y", -1)]
-    result = []
-    for source in (left, right, far):
-        quarters = source + [shift(source[1], "x", -1), shift(source[0], "x", 1)]
-        result.append([(quarter, shift(quarter, "core", 1)) for quarter in quarters])
-    return result
-
-
-def column_table(routes, route_weights, expert_count):
+    )(normed, hidden, weight_table, *own_weights, other_weights)
+
+
+def column_table(routes, route_weights, expert_count, n):
     experts = jnp.arange(expert_count, dtype=jnp.int32)
     chosen = routes[:, :, None] == experts[None, None, :]
     table = jnp.sum(jnp.where(chosen, route_weights[:, :, None], 0.0), axis=1)
-    table = lax.all_gather(table, "z")
-    n = lax.axis_size("z")
-    table = table.reshape(n, table.shape[1], expert_count // n, n)
-    mine = jnp.arange(n, dtype=jnp.int32) == lax.axis_index("z")
-    table = jnp.sum(jnp.where(mine, table, 0.0), axis=3)
-    count = expert_count // n
-    order = lax.rem(lax.axis_index("y") + jnp.array([0, count - 1, 1, 2], jnp.int32), count)
-    picks = order[:, None] == jnp.arange(count, dtype=jnp.int32)[None, :]
-    return jnp.sum(jnp.where(picks, table[:, :, None, :], 0.0), axis=3)
+    return jnp.transpose(table.reshape(table.shape[0], expert_count // n, n), (2, 0, 1))
 
 
 def body(
@@ -346,50 +538,50 @@
     routes,
     route_weights,
 ):
-    half_rows, stream_count, query_width = queries.shape
+    half_rows, stream_count, _ = queries.shape
     model_width = residual.shape[2]
     token_rows = half_rows * stream_count
     expert_count = lax.axis_size(EXPERT)
-    item_count = stream_count * HEADS // expert_count
+    items = stream_count * HEADS
+
+    def by_stream(array):
+        array = array.reshape(half_rows, stream_count, array.shape[-1])
+        return jnp.swapaxes(array, 0, 1).reshape(token_rows, array.shape[-1])
+
+    query_items = queries.reshape(half_rows, items, NOPE + ROPE)
+    rope_items = jnp.broadcast_to(key_rope[:, :, None, :], (half_rows, stream_count, HEADS, ROPE))
+    packed = jnp.concatenate(
+        [
+            query_items[:, :, :NOPE],
+            key_nope.reshape(half_rows, items, NOPE),
+            values.reshape(half_rows, items, V_DIM),
+            query_items[:, :, NOPE:],
+            rope_items.reshape(half_rows, items, ROPE),
+        ],
+        axis=2,
+    )
+    borders = jnp.sum((segments == 0).astype(jnp.int32), axis=1)
+    mine = jnp.arange(stream_count, dtype=jnp.int32) == lax.axis_index(EXPERT) // HEADS
+    bound = jnp.sum(jnp.where(mine, borders, 0)).reshape(1)
     own_weights = (expert_gate[0].T, expert_up[0].T, expert_down[0])
-    other_weights = column_weights(*own_weights)
-    weight_table = column_table(routes[0, 0], route_weights[0, 0], expert_count)
-    key_heads = jnp.concatenate(
-        [
-            key_nope.reshape(half_rows, stream_count, HEADS, NOPE),
-            jnp.broadcast_to(key_rope[:, :, None, :], (half_rows, stream_count, HEADS, ROPE)),
-        ],
-        axis=3,
+    table = column_table(
+        by_stream(routes[0, 0]), by_stream(route_weights[0, 0]), expert_count, lax.axis_size("z")
     )
-    query_items = queries.reshape(half_rows, stream_count * HEADS, NOPE + ROPE)
-    key_items = key_heads.reshape(half_rows, stream_count * HEADS, NOPE + ROPE)
-    value_items = values.reshape(half_rows, stream_count * HEADS, V_DIM)
-    query_all, key_all, value_all = side_by_side(
-        (query_items, key_items, value_items), EXPERT, 1, 0, 2
+    attn_rows, weight_table, other_weights = attend_and_gather(
+        jnp.swapaxes(packed, 0, 1), bound, table, own_weights
     )
-    item_ids = lax.axis_index(EXPERT) * item_count + jnp.arange(item_count, dtype=jnp.int32)
-    stream_ids = item_ids // HEADS
-    selector = (stream_ids[:, None] == jnp.arange(stream_count, dtype=jnp.int32)[None, :]).astype(
-        jnp.int32
-    )
-    segment_items = jnp.sum(selector[:, :, None] * segments[None, :, :], axis=1)
-    attended_items = attend_items(query_all, key_all, value_all, segment_items)
-    attended_back = lax.all_to_all(
-        attended_items, EXPERT, split_axis=0, concat_axis=1, tiled=True
-    )
-    attn_rows = attended_back.reshape(token_rows, HEADS * V_DIM)
     projected = jnp.dot(
         attn_rows,
         lax.all_gather(out_proj, DP + EXPERT, axis=0, tiled=True),
         preferred_element_type=jnp.float32,
     )
-    hidden = residual.reshape(token_rows, model_width).astype(jnp.float32) + projected
+    hidden = by_stream(residual).astype(jnp.float32) + projected
     mean_square = jnp.mean(hidden * hidden, axis=1, keepdims=True)
     normed = (hidden * lax.rsqrt(mean_square + EPSILON) * norm_gain.astype(jnp.float32)).astype(
         jnp.bfloat16
     )
     layer_out = mix_experts(normed, hidden, weight_table, own_weights, other_weights)
-    return layer_out.reshape(half_rows, stream_count, model_width)
+    return jnp.swapaxes(layer_out.reshape(stream_count, half_rows, model_width), 0, 1)
 
 
 def solution(mesh):

time: 361 us -> 287 us (0.80)
  Pallas kernels: 107 us -> 245 us
  waiting for transfers between devices: 117 us -> 0.68 us
  starting transfers between devices: 36.9 us -> 0.04 us
  blocking collectives: 32.9 us -> 0 us
  matrix products: 16.3 us -> 4.98 us
  other arithmetic: 7.37 us -> 2.34 us
  local copies, waits for them, and re-layouts: 24.2 us -> 19.4 us
    pallas_call x0 -> x1, Pallas kernels: none -> 138 us  [attend_and_gather(): pl.pallas_call(front_kernel, out_shape=(jax.ShapeDtypeStruct((peers // he...]
    ppermute x24 -> x0, waiting for transfers between devices: 116 us -> none  [shift(): return lax.ppermute(array, axis, [(i, (i + by) % n) for i in range(n)])]
    all_gather x1 -> x0, blocking collectives: 32.9 us -> none  [column_table(): table = lax.all_gather(table, 'z')]
    all_to_all x2 -> x0, starting transfers between devices: 18.9 us -> none  [the longest x1 11.5 us: side_by_side(): lax.all_to_all(both, axis, split_axis=split_dim, concat_axis=concat_dim,...]
    ppermute x24 -> x0, starting transfers between devices: 18 us -> none  [shift(): return lax.ppermute(array, axis, [(i, (i + by) % n) for i in range(n)])]
    dot_general x8 -> x0, matrix products: 11.5 us -> none  [the longest x4 6.16 us: one_block(): jnp.einsum('iqk,kid->qid', weights, value_items, preferred_element_type=j...]
    dynamic_slice x9 -> x0, local copies, waits for them, and re-layouts: 3.77 us -> none  [the longest x4 2.57 us: attend_items(): lax.map(one_block, jnp.arange(length // block_rows, dtype=jnp.int32))]
    reshape x5 -> x7, local copies, waits for them, and re-layouts: 5.51 us -> 8.9 us  [the longest x1 2.6 us: body(): query_items = queries.reshape(half_rows, items, NOPE + ROPE)]
  transfers between devices with their start and end apart: 27 -> 1, of which waited for: 8 -> 0; matrix products, arithmetic and copies ran while one was open for 12% -> 6% of each run, Pallas kernels for 0% -> 48%
where the time goes in v3:
time: 287 us; the launch traced here: 286 us
  Pallas kernels  245 us (85%)
  local copies, waits for them, and re-layouts  19.4 us (7%)
  between operations  13.6 us (5%)
  matrix products  4.98 us (2%)
    pallas_call x1, Pallas kernels, attend_and_gather(): pl.pallas_call(front_kernel, out_shape=(jax.ShapeDtypeStruct((peers // he...  138 us
    pallas_call x1, Pallas kernels, mix_experts(): pl.pallas_call(functools.partial(moe_kernel, n), out_shape=jax.ShapeDtype...  107 us
  transfers between devices with their start and end apart: 1, of which 0 were waited for; matrix products, arithmetic and copies ran while one was open for 6% of the time, Pallas kernels for 48%

profile of v3, /device:TPU:2, one launch (start us, length us, event | category | flops | bytes accessed | tf_op | source)
XLA Modules:
  0.0 286.1 jit_solution(1770549535777040014)
XLA Ops:
  6.5 0.0 copy-start.3
  6.5 0.0 copy-start.4
  6.5 0.0 copy-start.7
  6.5 0.0 copy-start.8
  6.5 0.0 copy-start.2
  6.5 0.0 copy-start.6
  6.6 0.0 all-gather.2.cloned.1.call-start
  6.6 0.7 all-gather.2.cloned.1.call-update
  7.3 2.6 reshape.36
  9.9 0.1 slice.8
  10.0 0.0 copy-start.5
  10.0 0.1 slice.9
  10.1 0.2 copy.43
  10.4 1.0 copy.44
  11.4 1.4 reshape.37
  12.7 1.0 copy.35
  13.7 0.0 copy-done.3
  13.7 0.3 reshape.38
  14.1 1.0 copy.36
  15.1 0.0 copy-done.4
  15.1 0.0 copy-done.7
  15.1 0.1 copy.39
  15.2 0.1 copy.40
  15.3 0.1 broadcast_in_dim.29
  15.4 0.0 copy-done.8
  15.4 0.1 copy.37
  15.5 0.1 copy.38
  15.6 0.1 eq.31
  15.7 0.2 copy.41
  15.9 0.0 copy-done.2
  15.9 0.6 convert_bitcast_fusion
  16.5 1.6 copy.31
  18.1 0.0 copy-done.6
  18.1 0.9 broadcast_in_dim.27
  19.0 4.2 %concatenate.3 = bf16[64,32,512]{2,0,1:T(8,128)(2,1)S(1)} concatenate(bf16[64,32,128]{2,0,1:T(8,128)(2,1)S(1)} %copy.43, bf16[64,32,128]{2,0,1:T(8,128)(2,1)} %copy.35, bf16[64,32,128]{2,0,1:T(8,128)(2,1)} %copy.36, bf16[64,32,64]{2,0,1:T(8,128)(2,1)} %copy.44, bf16[64,32,64]{2,0,1:T(8,128)(2,1)} %bitcast.34), dimensions={2} | concatenate | bytes 4194304 | tf_op jit(solution)/shard_map/concatenate | solution.py:553
  23.3 0.0 copy-done.5
  23.3 0.1 fusion
  23.4 0.6 fusion.1
  24.1 138.5 %shard_map.127 = (bf16[128,2048]{1,0:T(8,128)(2,1)S(1)}, f32[8,128,4]{2,1,0:T(8,128)S(1)}, bf16[3,3,704,2048]{3,2,1,0:T(8,128)(2,1)}) custom-call(bf16[32,64,512]{2,1,0:T(8,128)(2,1)S(1)} %bitcast.31, s32[1]{0:T(128)} %bitcast.4.bound, f32[8,128,4]{2,1,0:T(8,128)S(1)} %bitcast.32, bf16[704,2048]{1,0:T(8,128)(2,1)} %bitcast.39, bf16[704,2048]{1,0:T(8,128)(2,1)} %bitcast.41, ...), custom_call_target="tpu_custom_call" | custom-call | flops 99999997952 | bytes 40000000 | tf_op jit(solution)/shard_map/pallas_call | solution.py:261
  162.6 0.0 copy-start
  162.6 0.8 copy-done
  163.4 0.0 all-gather.2.cloned.1.call-done
  163.4 5.0 %multiply_reduce_fusion = (f32[128]{0:T(128)S(1)}, f32[128,2048]{1,0:T(8,128)S(1)}) fusion(f32[128,2048]{1,0:T(8,128)} %bitcast.33, bf16[128,2048]{1,0:T(8,128)(2,1)S(1)} %get-tuple-element.8, bf16[2048,2048]{1,0:T(8,128)(2,1)} %all-gather.2.cloned.1.call-done), kind=kOutput, calls=%fused_computation.3 | convolution fusion | flops 1074528128 | bytes 11010560 | tf_op jit(solution)/shard_map/dot_general | solution.py:573
  168.3 0.0 copy-start.1
  168.4 1.0 copy-done.1
  169.3 1.0 multiply_convert_fusion.x_ref
  170.3 106.6 %shard_map.128 = bf16[128,2048]{1,0:T(8,128)(2,1)} custom-call(bf16[128,2048]{1,0:T(8,128)(2,1)} %multiply_convert_fusion.x_ref, f32[128,2048]{1,0:T(8,128)} %copy-done.1, f32[8,128,4]{2,1,0:T(8,128)} %copy-done, bf16[704,2048]{1,0:T(8,128)(2,1)} %bitcast.40, bf16[704,2048]{1,0:T(8,128)(2,1)} %bitcast.42, bf16[704,2048]{1,0:T(8,128)(2,1)} %bitcast.44, ...), custom_call_target="tpu_custom_call" | custom-call | flops 35433480192 | bytes 40000000 | tf_op jit(solution)/shard_map/pallas_call | solution.py:493
  276.8 2.4 copy.46
  (4 shorter events, 0.0 us)
Async XLA Ops:
  6.5 7.2 %copy-start.3 = (bf16[64,2,2048]{2,1,0:T(2,128)(2,1)S(1)}, bf16[64,2,2048]{2,1,0:T(2,128)(2,1)}, u32[]{:S(2)}) copy-start(bf16[64,2,2048]{2,1,0:T(2,128)(2,1)} %param.16) | copy-start | bytes 1572868
  6.5 8.5 %copy-start.4 = (bf16[64,2,64]{2,1,0:T(2,128)(2,1)S(1)}, bf16[64,2,64]{2,1,0:T(2,128)(2,1)}, u32[]{:S(2)}) copy-start(bf16[64,2,64]{2,1,0:T(2,128)(2,1)} %param.15) | copy-start | bytes 49156
  6.5 8.5 %copy-start.7 = (f32[1,1,128,6]{2,1,3,0:T(1,128)S(1)}, f32[1,1,128,6]{2,1,3,0:T(1,128)}, u32[]{:S(2)}) copy-start(f32[1,1,128,6]{2,1,3,0:T(1,128)} %param.25) | copy-start | bytes 9220
  6.5 8.8 %copy-start.8 = (s32[1,1,128,6]{2,1,3,0:T(1,128)S(1)}, s32[1,1,128,6]{2,1,3,0:T(1,128)}, u32[]{:S(2)}) copy-start(s32[1,1,128,6]{2,1,3,0:T(1,128)} %param.24) | copy-start | bytes 9220
  6.5 9.4 %copy-start.2 = (bf16[64,2,2048]{2,1,0:T(2,128)(2,1)S(1)}, bf16[64,2,2048]{2,1,0:T(2,128)(2,1)}, u32[]{:S(2)}) copy-start(bf16[64,2,2048]{2,1,0:T(2,128)(2,1)} %param.17) | copy-start | bytes 1572868
  6.5 11.6 %copy-start.6 = (bf16[2048]{0:T(1024)(128)(2,1)S(1)}, bf16[2048]{0:T(1024)(128)(2,1)}, u32[]{:S(2)}) copy-start(bf16[2048]{0:T(1024)(128)(2,1)} %param.20) | copy-start | bytes 12292
  6.6 156.8 %all-gather.2.cloned.1.call-start = ((), (), s32[]{:S(2)}) async-start(), calls=%async_computation | async-start | bytes 8421376 | tf_op jit(solution)/shard_map/all_gather | solution.py:575
  10.0 13.3 %copy-start.5 = (s32[2,2048]{1,0:T(2,128)S(1)}, s32[2,2048]{1,0:T(2,128)}, u32[]{:S(2)}) copy-start(s32[2,2048]{1,0:T(2,128)} %param.18) | copy-start | bytes 49156
  162.6 0.8 copy-start
  168.3 1.0 copy-start.1
Sparse Core Ops, SparseCore 0:
  11.1 135.7 all-gather.1

commit v4 on v3

--- a/solution.py
+++ b/solution.py
@@ -22,9 +22,10 @@
 QUERY_BLOCK = 512
 
 
-def front_kernel(qkv, bound, table, own_g, own_u, own_d, attn_ref, tab_ref, others,
+def front_kernel(queries, keys, values, ropes, bound, table, proj, own_g, own_u, own_d,
+                 attn_ref, tab_ref, others, proj_all,
                  rows_buf, qbuf, kbuf, att, local_sem, a2a_sem, att_sem, tab_sem,
-                 ysend, yrecv, fsend, frecv, xsend, xrecv, csend, crecv):
+                 ysend, yrecv, xsend, xrecv, csend, crecv, psend, precv):
     size_x, size_y, size_z = lax.axis_size("x"), lax.axis_size("y"), lax.axis_size("z")
     peers = size_y * size_z
     x, core = lax.axis_index("x"), lax.axis_index("core")
@@ -33,7 +34,8 @@
     up_y, down_y = {"y": lax.rem(y + 1, size_y)}, {"y": lax.rem(y + size_y - 1, size_y)}
     up_x, down_x = {"x": lax.rem(x + 1, size_x)}, {"x": lax.rem(x + size_x - 1, size_x)}
     other_core = {"core": 1 - core}
-    block = qkv.shape[1]
+    packed = (queries, keys, values, ropes)
+    block = queries.shape[1]
     heads = attn_ref.shape[1] // V_DIM
     ff, width = own_d.shape
     high, wide = ff // size_x, width // 4
@@ -57,17 +59,42 @@
         pl.semaphore_signal(barrier, inc=1, device_id=device, device_id_type=MESH)
     pl.semaphore_wait(barrier, peers + 2)
 
+    def blocks(first, amount):
+        return proj_all.at[pl.ds(first, amount)]
+
+    own_block = ((x * 2 + core) * size_y + y) * size_z + z
+    group = peers
+
+    def group_of(gx, gcore):
+        return (lax.rem(gx + size_x, size_x) * 2 + gcore) * group
+
+    def proj_copy(n, first, amount, device):
+        return remote(blocks(first, amount), blocks(first, amount), psend.at[n], precv.at[n], device)
+
+    for d in range(1, size_z):
+        remote(proj, proj_all.at[own_block], psend.at[0], precv.at[0], {"z": lax.rem(z + d, size_z)}).start()
+    own_proj = pltpu.make_async_copy(proj, proj_all.at[own_block], local_sem.at[3])
+    own_proj.start()
+
     def rows_of(e):
         return pl.ds(pl.multiple_of(e * block, block), block)
 
     def send_rows(d, carry):
         e = lax.rem(me + d, peers)
-        remote(qkv.at[e], rows_buf.at[rows_of(me)], a2a_sem.at[0], a2a_sem.at[1], peer(e)).start()
+        for i, part in enumerate(packed):
+            place = rows_buf.at[rows_of(me), pl.ds(i * 128, 128)]
+            remote(part.at[e], place, a2a_sem.at[0], a2a_sem.at[1], peer(e)).start()
         return carry
 
     lax.fori_loop(1, peers, send_rows, 0)
-    own_rows = pltpu.make_async_copy(qkv.at[me], rows_buf.at[rows_of(me)], local_sem.at[0])
-    own_rows.start()
+    for i, part in enumerate(packed):
+        place = rows_buf.at[rows_of(me), pl.ds(i * 128, 128)]
+        pltpu.make_async_copy(part.at[me], place, local_sem.at[0]).start()
+
+    own_proj.wait()
+    proj_copy(0, 0, size_z - 1, up_y).wait_recv()
+    for d in range(1, size_y):
+        proj_copy(1, own_block - z, size_z, {"y": lax.rem(y + d, size_y)}).start()
 
     def columns(u):
         return pl.ds(pl.multiple_of((core * 2 + u) * wide, wide), wide)
@@ -94,11 +121,6 @@
         n = y_index(s, q, u)
         return remote(region(s, q, u), region(s, q, u), ysend.at[n], yrecv.at[n], up_y)
 
-    def f_copy(q, u):
-        source, device = (0, up_y) if q == 0 else (1, down_y)
-        n = q * 2 + u
-        return remote(region(source, q, u), region(2, q, u), fsend.at[n], frecv.at[n], device)
-
     def x_copy(s, q, u):
         device, slot = (up_x, 3) if q == 0 else (down_x, 2)
         n = (s * 2 + q) * 2 + u
@@ -122,6 +144,10 @@
     own_table = pltpu.make_async_copy(table.at[z], tab_ref.at[z], local_sem.at[1])
     own_table.start()
 
+    proj_copy(1, 0, (size_y - 1) * size_z, up_y).wait_recv()
+    for n, device in ((2, up_x), (3, down_x), (4, other_core)):
+        proj_copy(n, group_of(x, core), group, device).start()
+
     def arrived(s, q, u):
         x_copy(s, q, u).start()
         c_copy(s, q, u).start()
@@ -129,10 +155,18 @@
     for u in range(2):
         for s in range(2):
             y_copy(s, s, u).wait_recv()
-            f_copy(s, u).start()
             arrived(s, s, u)
 
-    own_rows.wait()
+    half_group = group // 2
+    proj_copy(2, group_of(x - 1, core), group, up_x).wait_recv()
+    proj_copy(5, group_of(x - 1, core), half_group, up_x).start()
+    proj_copy(7, group_of(x - 1, core), group, other_core).start()
+    proj_copy(3, group_of(x + 1, core), group, up_x).wait_recv()
+    proj_copy(6, group_of(x + 1, core) + half_group, half_group, down_x).start()
+    proj_copy(8, group_of(x + 1, core), group, other_core).start()
+
+    own_place = rows_buf.at[rows_of(me)]
+    pltpu.make_async_copy(own_place, own_place, local_sem.at[0]).wait()
     most = rows_buf.at[pl.ds(0, (peers - 1) * block)]
     remote(most, most, a2a_sem.at[0], a2a_sem.at[1], up_y).wait_recv()
 
@@ -216,21 +250,18 @@
         x_copy(s, q, u).wait_recv()
         c_copy(s, 3 if q == 0 else 2, u).start()
 
+    proj_copy(5, 0, half_group, up_x).wait_recv()
+    proj_copy(9, group_of(x + 2, core), half_group, other_core).start()
+    proj_copy(6, 0, half_group, up_x).wait_recv()
+    proj_copy(10, group_of(x + 2, core) + half_group, half_group, other_core).start()
     for u in range(2):
         for s in range(2):
             crossed(s, s, u)
     for u in range(2):
-        for q in range(2):
-            f_copy(q, u).wait_recv()
-            arrived(2, q, u)
-    for u in range(2):
         for s in range(2):
             crossed(s, 1 - s, u)
-    for u in range(2):
-        for q in range(2):
-            crossed(2, q, u)
-
-    for s in range(3):
+
+    for s in range(2):
         for q in range(4):
             for u in range(2):
                 c_copy(s, q, u).wait()
@@ -238,9 +269,13 @@
         for q in range(2):
             for s in range(2):
                 y_copy(s, q, u).wait_send()
-            f_copy(q, u).wait_send()
-            for s in range(3):
                 x_copy(s, q, u).wait_send()
+    proj_copy(0, 0, size_z - 1, up_y).wait_send()
+    proj_copy(1, 0, (size_y - 1) * size_z, up_y).wait_send()
+    for n, amount in ((2, group), (3, group), (5, half_group), (6, half_group)):
+        proj_copy(n, 0, amount, up_x).wait_send()
+    for n, amount in ((4, group), (7, group), (8, group), (9, half_group), (10, half_group)):
+        proj_copy(n, 0, amount, other_core).wait()
     remote(most, most, a2a_sem.at[0], a2a_sem.at[1], up_y).wait_send()
     local_back().wait()
     back = att.at[pl.ds(0, (peers - 1) * block)]
@@ -250,8 +285,8 @@
     remote(tables, tables, tab_sem.at[0], tab_sem.at[1], up_y).wait()
 
 
-def attend_and_gather(qkv, bound, table, own_weights):
-    peers, block, packed = qkv.shape
+def attend_and_gather(packed, bound, table, proj, own_weights):
+    peers, block, _ = packed[0].shape
     ff, width = own_weights[2].shape
     heads = width // V_DIM
     length = peers * block
@@ -263,37 +298,39 @@
         out_shape=(
             jax.ShapeDtypeStruct((peers // heads * block, width), jnp.bfloat16),
             jax.ShapeDtypeStruct(table.shape, jnp.float32),
-            jax.ShapeDtypeStruct((3, 3, ff, width), jnp.bfloat16),
+            jax.ShapeDtypeStruct((2, 3, ff, width), jnp.bfloat16),
+            jax.ShapeDtypeStruct((width // proj.shape[0],) + proj.shape, jnp.bfloat16),
         ),
-        in_specs=[anywhere, pl.BlockSpec(memory_space=pltpu.SMEM), vmem] + [anywhere] * 3,
-        out_specs=(vmem, vmem, anywhere),
+        in_specs=[anywhere] * 4 + [pl.BlockSpec(memory_space=pltpu.SMEM), vmem] + [anywhere] * 4,
+        out_specs=(vmem, vmem, anywhere, anywhere),
         scratch_shapes=[
-            pltpu.VMEM((length, packed), jnp.bfloat16),
+            pltpu.VMEM((length, 512), jnp.bfloat16),
             pltpu.VMEM((length, 256), jnp.bfloat16),
             pltpu.VMEM((length, 256), jnp.bfloat16),
             pltpu.VMEM((length, V_DIM), jnp.bfloat16),
-            dma((3,)),
+            dma((4,)),
             dma((2,)),
             dma((2,)),
             dma((2,)),
             dma((8,)),
             dma((8,)),
-            dma((4,)),
-            dma((4,)),
-            dma((12,)),
-            dma((12,)),
-            dma((24,)),
-            dma((24,)),
+            dma((8,)),
+            dma((8,)),
+            dma((16,)),
+            dma((16,)),
+            dma((11,)),
+            dma((11,)),
         ],
         compiler_params=pltpu.CompilerParams(
             collective_id=1, has_side_effects=True, vmem_limit_bytes=50000000
         ),
         cost_estimate=pl.CostEstimate(flops=100000000000, bytes_accessed=40000000, transcendentals=0),
-    )(qkv, bound, table, *own_weights)
+    )(*packed, bound, table, proj, *own_weights)
 
 
 def moe_kernel(axis_size, x_ref, hid_ref, wt_ref, own_g, own_u, own_d, others,
-               out_ref, xbuf, acc, act, weights, rbuf, lbuf, start_sem, send_sem, recv_sem, wsem):
+               out_ref, xbuf, acc, act, weights, rbuf, lbuf, start_sem, send_sem, recv_sem, wsem,
+               fsend, frecv, xsend, xrecv, csend, crecv):
     n = axis_size
     half_n = n // 2
     y, z = lax.axis_index("y"), lax.axis_index("z")
@@ -312,13 +349,19 @@
 
     for i, own in enumerate((own_g, own_u, own_d)):
         pltpu.make_async_copy(own, weights.at[0, i], wsem.at[0]).start()
-    for k in range(1, count):
+    last = count - 1
+    for k in range(1, last):
         pltpu.make_async_copy(others.at[k - 1], weights.at[k], wsem.at[k]).start()
 
+    size_x, size_y = lax.axis_size("x"), lax.axis_size("y")
+    x, core = lax.axis_index("x"), lax.axis_index("core")
+    up_y, down_y = {"y": lax.rem(y + 1, size_y)}, {"y": lax.rem(y + size_y - 1, size_y)}
+    up_x, down_x = {"x": lax.rem(x + 1, size_x)}, {"x": lax.rem(x + size_x - 1, size_x)}
+    other_core = {"core": 1 - core}
     barrier = pltpu.get_barrier_semaphore()
-    for neighbour in (left, right):
+    for neighbour in (left, right, up_y, down_y, up_x, down_x, other_core):
         pl.semaphore_signal(barrier, inc=1, device_id=neighbour, device_id_type=MESH)
-    pl.semaphore_wait(barrier, 2)
+    pl.semaphore_wait(barrier, 7)
 
     def gather_copy(j, way):
         d = j // 2
@@ -353,6 +396,48 @@
         for way in range(2):
             gather_copy(j, way).start()
 
+    high, wide = ff // size_x, width // 4
+
+    def section(ref, k, q, u):
+        columns = pl.ds(pl.multiple_of((core * 2 + u) * wide, wide), wide)
+        return ref.at[k, :, pl.ds(q * high, high), columns]
+
+    def remote(src, dst, send, recv, device):
+        return pltpu.make_async_remote_copy(
+            src_ref=src, dst_ref=dst, send_sem=send, recv_sem=recv, device_id=device, device_id_type=MESH
+        )
+
+    def f_copy(q, u):
+        n = q * 2 + u
+        return remote(
+            section(others, q, q, u), section(weights, last, q, u), fsend.at[n], frecv.at[n],
+            up_y if q == 0 else down_y,
+        )
+
+    def x_copy(q, u):
+        n = q * 2 + u
+        device, slot = (up_x, 3) if q == 0 else (down_x, 2)
+        return remote(section(weights, last, q, u), section(weights, last, slot, u), xsend.at[n], xrecv.at[n], device)
+
+    def c_copy(q, u):
+        n = q * 2 + u
+        return remote(section(weights, last, q, u), section(weights, last, q, u), csend.at[n], crecv.at[n], other_core)
+
+    def arrived(u):
+        for q in range(2):
+            f_copy(q, u).wait_recv()
+            x_copy(q, u).start()
+            c_copy(q, u).start()
+
+    def crossed(u):
+        for q in range(2):
+            x_copy(q, u).wait_recv()
+            c_copy(3 if q == 0 else 2, u).start()
+
+    for u in range(2):
+        for q in range(2):
+            f_copy(q, u).start()
+
     def pass_on(j):
         for way in range(2):
             gather_arrival(j, way).wait_recv()
@@ -382,17 +467,19 @@
             a = g / (1.0 + jnp.exp(-g)) * u * scale
             act[k, 0:m, lo:hi] = a.astype(jnp.bfloat16)
 
-    def down(slots):
+    def down(slots, experts, more):
         m = rows * len(slots)
 
         def columns(q, carry):
             span = pl.ds(pl.multiple_of(q * 512, min(512, width)), min(512, width))
-            y = jnp.dot(act[0, 0:m, :], weights[0, 2, :, span], preferred_element_type=jnp.float32)
-            for k in range(1, count):
+            y = jnp.dot(act[experts[0], 0:m, :], weights[experts[0], 2, :, span], preferred_element_type=jnp.float32)
+            for k in experts[1:]:
                 y += jnp.dot(act[k, 0:m, :], weights[k, 2, :, span], preferred_element_type=jnp.float32)
-            y = y.astype(jnp.bfloat16)
             for i, s in enumerate(slots):
-                acc[s, :, span] = y[i * rows:(i + 1) * rows]
+                part_y = y[i * rows:(i + 1) * rows]
+                if more:
+                    part_y += acc[s, :, span].astype(jnp.float32)
+                acc[s, :, span] = part_y.astype(jnp.bfloat16)
             return carry
 
         lax.fori_loop(0, max(1, width // 512), columns, 0)
@@ -411,8 +498,10 @@
 
         return carry
 
-    lax.fori_loop(0, count, own_step, 0)
-    down([z])
+    early = tuple(range(last))
+    lax.fori_loop(0, last, own_step, 0)
+    down([z], early, False)
+    arrived(0)
 
     def pair_step(p, carry):
         pass_on(2 * p - 1)
@@ -427,8 +516,21 @@
 
             return inner
 
-        lax.fori_loop(0, count, one, 0)
-        down(slots)
+        lax.fori_loop(0, last, one, 0)
+        down(slots, early, False)
+
+        @pl.when(p == 1)
+        def _():
+            arrived(1)
+
+        @pl.when(p == 2)
+        def _():
+            crossed(0)
+
+        @pl.when(p == 3)
+        def _():
+            crossed(1)
+
         return carry
 
     lax.fori_loop(1, half_n, pair_step, 0)
@@ -438,12 +540,17 @@
         gate_up(far, k)
         return carry
 
-    lax.fori_loop(0, count, far_step, 0)
-    down(far)
-    for j in range(sent):
-        for way in range(2):
-            gather_copy(j, way).wait_send()
-
+    lax.fori_loop(0, last, far_step, 0)
+    down(far, early, False)
+    for q in range(4):
+        for u in range(2):
+            c_copy(q, u).wait_recv()
+
+    def finish(slots):
+        gate_up(slots, last)
+        down(slots, (last,), True)
+
+    finish(far)
     bufs = (rbuf, lbuf)
 
     def sum_copy(j, way):
@@ -456,7 +563,7 @@
             device_id_type=MESH,
         )
 
-    for j in range(sent):
+    def send_sums(j):
         for way in range(2):
             off = half_n - (j + 1) // 2
             owner = slot(n - off) if way == 0 else slot(off)
@@ -468,6 +575,14 @@
                 sum_copy(j - 2, way).wait_recv()
                 bufs[way][j - 2] = (bufs[way][j - 2].astype(jnp.float32) + own_part.astype(jnp.float32)).astype(jnp.bfloat16)
             sum_copy(j, way).start()
+
+    send_sums(0)
+    for p in range(half_n - 1, 0, -1):
+        finish([slot(p), slot(n - p)])
+        j = 2 * (half_n - p) - 1
+        send_sums(j)
+        send_sums(j + 1)
+    finish([z])
     for way in range(2):
         for j in (sent - 2, sent - 1):
             sum_copy(j, way).wait_recv()
@@ -479,14 +594,21 @@
         out_ref[part(c)] = total.astype(jnp.bfloat16)
     for j in range(sent):
         for way in range(2):
+            gather_copy(j, way).wait_send()
             sum_copy(j, way).wait_send()
+    for q in range(4):
+        for u in range(2):
+            c_copy(q, u).wait_send()
+            if q < 2:
+                f_copy(q, u).wait_send()
+                x_copy(q, u).wait_send()
 
 
 def mix_experts(normed, hidden, weight_table, own_weights, other_weights):
     rows, width = normed.shape
     n = lax.axis_size("z")
     ff = own_weights[2].shape[0]
-    count = 1 + other_weights.shape[0]
+    count = 2 + other_weights.shape[0]
     sent = n - 1
     vmem = pl.BlockSpec(memory_space=pltpu.VMEM)
     anywhere = pl.BlockSpec(memory_space=pl.ANY)
@@ -506,6 +628,9 @@
             pltpu.SemaphoreType.DMA((2, 2 * sent)),
             pltpu.SemaphoreType.DMA((2, 2 * sent)),
             pltpu.SemaphoreType.DMA((count,)),
+        ] + [pltpu.SemaphoreType.DMA((4,))] * 4 + [
+            pltpu.SemaphoreType.DMA((8,)),
+            pltpu.SemaphoreType.DMA((8,)),
         ],
         compiler_params=pltpu.CompilerParams(
             collective_id=0, has_side_effects=True, vmem_limit_bytes=66000000
@@ -550,16 +675,18 @@
 
     query_items = queries.reshape(half_rows, items, NOPE + ROPE)
     rope_items = jnp.broadcast_to(key_rope[:, :, None, :], (half_rows, stream_count, HEADS, ROPE))
-    packed = jnp.concatenate(
-        [
+    ropes = jnp.concatenate(
+        [query_items[:, :, NOPE:], rope_items.reshape(half_rows, items, ROPE)], axis=2
+    )
+    packed = [
+        jnp.swapaxes(part, 0, 1)
+        for part in (
             query_items[:, :, :NOPE],
             key_nope.reshape(half_rows, items, NOPE),
             values.reshape(half_rows, items, V_DIM),
-            query_items[:, :, NOPE:],
-            rope_items.reshape(half_rows, items, ROPE),
-        ],
-        axis=2,
-    )
+            ropes,
+        )
+    ]
     borders = jnp.sum((segments == 0).astype(jnp.int32), axis=1)
     mine = jnp.arange(stream_count, dtype=jnp.int32) == lax.axis_index(EXPERT) // HEADS
     bound = jnp.sum(jnp.where(mine, borders, 0)).reshape(1)
@@ -567,13 +694,11 @@
     table = column_table(
         by_stream(routes[0, 0]), by_stream(route_weights[0, 0]), expert_count, lax.axis_size("z")
     )
-    attn_rows, weight_table, other_weights = attend_and_gather(
-        jnp.swapaxes(packed, 0, 1), bound, table, own_weights
+    attn_rows, weight_table, other_weights, proj_all = attend_and_gather(
+        packed, bound, table, out_proj, own_weights
     )
     projected = jnp.dot(
-        attn_rows,
-        lax.all_gather(out_proj, DP + EXPERT, axis=0, tiled=True),
-        preferred_element_type=jnp.float32,
+        attn_rows, proj_all.reshape(model_width, model_width), preferred_element_type=jnp.float32
     )
     hidden = by_stream(residual).astype(jnp.float32) + projected
     mean_square = jnp.mean(hidden * hidden, axis=1, keepdims=True)

time: 287 us -> 259 us (0.902)
  between operations: 13.6 us -> 0.26 us
  local copies, waits for them, and re-layouts: 19.4 us -> 9.68 us
  Pallas kernels: 245 us -> 240 us
    concatenate x1 -> x0, local copies, waits for them, and re-layouts: 4.25 us -> none  [body(): jnp.concatenate([query_items[:, :, :NOPE], key_nope.reshape(half_rows, it...]
    pallas_call x1, Pallas kernels: 138 us -> 135 us  [attend_and_gather(): pl.pallas_call(front_kernel, out_shape=(jax.ShapeDtypeStruct((peers // he...]
  transfers between devices with their start and end apart: 1 -> 0, of which waited for: 0 -> 0; matrix products, arithmetic and copies ran while one was open for 6% -> 0% of each run, Pallas kernels for 48% -> 0%
where the time goes in v4:
time: 259 us
  Pallas kernels  240 us (93%)
  local copies, waits for them, and re-layouts  9.68 us (4%)
  matrix products  4.81 us (2%)
  other arithmetic  3.64 us (1%)
    pallas_call x1, Pallas kernels, attend_and_gather(): pl.pallas_call(front_kernel, out_shape=(jax.ShapeDtypeStruct((peers // he...  135 us
    pallas_call x1, Pallas kernels, mix_experts(): pl.pallas_call(functools.partial(moe_kernel, n), out_shape=jax.ShapeDtype...  105 us

profile of v4, /device:TPU:2, one launch (start us, length us, event | category | flops | bytes accessed | tf_op | source)
XLA Modules:
  0.0 258.7 jit_solution(2894182889279769256)
XLA Ops:
  0.0 0.0 copy-start.4
  0.0 0.0 copy-start.5
  0.0 0.0 copy-start.7
  0.0 0.0 copy-start.8
  0.0 0.0 copy-start
  0.0 0.9 fusion.5
  1.0 0.6 fusion.6
  1.6 2.6 %reshape.39 = bf16[64,32,192]{2,1,0:T(8,128)(2,1)S(1)} reshape(bf16[64,2,3072]{2,1,0:T(2,128)(2,1)} %param.13) | data formatting | bytes 1572864 | tf_op jit(solution)/shard_map/reshape | solution.py:676
  4.2 0.1 slice.9
  4.3 0.2 copy.44
  4.5 0.1 slice.8
  4.6 0.8 copy.36
  5.4 0.1 broadcast_in_dim.27
  5.5 0.5 maximum_bitcast_fusion
  6.0 0.0 copy-done.4
  6.0 0.3 reshape.40
  6.4 0.0 copy-done.5
  6.4 0.3 reshape.41
  6.7 0.4 copy_bitcast_fusion.2
  7.1 0.0 copy-done.7
  7.1 0.1 copy.39
  7.3 0.1 copy.40
  7.3 0.1 broadcast_in_dim.29
  7.4 0.0 copy-done.8
  7.4 0.1 copy.37
  7.5 0.1 copy.38
  7.6 0.1 eq.31
  7.7 0.2 copy.41
  8.0 0.0 copy-done
  8.0 0.0 copy-start.3
  8.0 134.9 %shard_map.127 = (bf16[128,2048]{1,0:T(8,128)(2,1)S(1)}, f32[8,128,4]{2,1,0:T(8,128)S(1)}, bf16[2,3,704,2048]{3,2,1,0:T(8,128)(2,1)}, bf16[256,8,2048]{2,1,0:T(8,128)(2,1)}) custom-call(bf16[32,64,128]{2,1,0:T(8,128)(2,1)S(1)} %get-tuple-element.16.queries, bf16[32,64,128]{2,1,0:T(8,128)(2,1)S(1)} %get-tuple-element.18.keys, ...), custom_call_target="tpu_custom_call" | custom-call | flops 99999997952 | bytes 40000000 | tf_op jit(solution)/shard_map/pallas_call | solution.py:296
  142.9 0.0 copy-start.1
  142.9 0.0 copy-done.3
  142.9 0.6 convert_bitcast_fusion
  143.5 0.6 copy.31
  144.2 0.0 copy-start.6
  144.2 4.8 %multiply_reduce_fusion = (f32[128]{0:T(128)S(1)}, f32[128,2048]{1,0:T(8,128)S(1)}) fusion(f32[128,2048]{1,0:T(8,128)S(1)} %bitcast.45, bf16[128,2048]{1,0:T(8,128)(2,1)S(1)} %get-tuple-element.9, bf16[256,8,2048]{2,1,0:T(8,128)(2,1)} %get-tuple-element.10), kind=kOutput, calls=%fused_computation.5 | convolution fusion | flops 1074528128 | bytes 11010560 | tf_op jit(solution)/shard_map/dot_general | solution.py:700
  149.0 0.0 copy-done.1
  149.0 0.0 copy-start.2
  149.0 0.0 copy-done.6
  149.0 0.9 copy-done.2
  150.0 1.0 multiply_convert_fusion.x_ref
  150.9 105.4 %shard_map.128 = bf16[128,2048]{1,0:T(8,128)(2,1)} custom-call(bf16[128,2048]{1,0:T(8,128)(2,1)} %multiply_convert_fusion.x_ref, f32[128,2048]{1,0:T(8,128)} %copy-done.2, f32[8,128,4]{2,1,0:T(8,128)} %copy-done.1, bf16[704,2048]{1,0:T(8,128)(2,1)} %bitcast.52, bf16[704,2048]{1,0:T(8,128)(2,1)} %bitcast.54, bf16[704,2048]{1,0:T(8,128)(2,1)} %bitcast.56, ...), custom_call_target="tpu_custom_call" | custom-call | flops 35433480192 | bytes 40000000 | tf_op jit(solution)/shard_map/pallas_call | solution.py:615
  256.3 2.4 copy.49
  (3 shorter events, 0.0 us)
Async XLA Ops:
  0.0 6.0 %copy-start.4 = (bf16[64,2,2048]{2,1,0:T(2,128)(2,1)S(1)}, bf16[64,2,2048]{2,1,0:T(2,128)(2,1)}, u32[]{:S(2)}) copy-start(bf16[64,2,2048]{2,1,0:T(2,128)(2,1)} %param.14) | copy-start | bytes 1572868
  0.0 6.4 %copy-start.5 = (bf16[64,2,2048]{2,1,0:T(2,128)(2,1)S(1)}, bf16[64,2,2048]{2,1,0:T(2,128)(2,1)}, u32[]{:S(2)}) copy-start(bf16[64,2,2048]{2,1,0:T(2,128)(2,1)} %param.16) | copy-start | bytes 1572868
  0.0 7.1 %copy-start.7 = (f32[1,1,128,6]{2,1,3,0:T(1,128)S(1)}, f32[1,1,128,6]{2,1,3,0:T(1,128)}, u32[]{:S(2)}) copy-start(f32[1,1,128,6]{2,1,3,0:T(1,128)} %param.25) | copy-start | bytes 9220
  0.0 7.4 %copy-start.8 = (s32[1,1,128,6]{2,1,3,0:T(1,128)S(1)}, s32[1,1,128,6]{2,1,3,0:T(1,128)}, u32[]{:S(2)}) copy-start(s32[1,1,128,6]{2,1,3,0:T(1,128)} %param.24) | copy-start | bytes 9220
  0.0 8.0 %copy-start = (bf16[8,2048]{1,0:T(8,128)(2,1)S(1)}, bf16[8,2048]{1,0:T(8,128)(2,1)}, u32[]{:S(2)}) copy-start(bf16[8,2048]{1,0:T(8,128)(2,1)} %proj.1) | copy-start | bytes 98308
  8.0 134.9 %copy-start.3 = (bf16[64,2,2048]{2,1,0:T(2,128)(2,1)S(1)}, bf16[64,2,2048]{2,1,0:T(2,128)(2,1)}, u32[]{:S(2)}) copy-start(bf16[64,2,2048]{2,1,0:T(2,128)(2,1)} %param.17) | copy-start | bytes 1572868
  142.9 6.1 %copy-start.1 = (f32[8,128,4]{2,1,0:T(8,128)}, f32[8,128,4]{2,1,0:T(8,128)S(1)}, u32[]{:S(2)}) copy-start(f32[8,128,4]{2,1,0:T(8,128)S(1)} %get-tuple-element.11.wt_ref) | copy-start | bytes 49156
  144.2 4.9 %copy-start.6 = (bf16[2048]{0:T(1024)(128)(2,1)S(1)}, bf16[2048]{0:T(1024)(128)(2,1)}, u32[]{:S(2)}) copy-start(bf16[2048]{0:T(1024)(128)(2,1)} %param.20) | copy-start | bytes 12292
  149.0 1.0 copy-start.2

commit v5 on v4

--- a/solution.py
+++ b/solution.py
@@ -149,8 +149,9 @@
         proj_copy(n, group_of(x, core), group, device).start()
 
     def arrived(s, q, u):
-        x_copy(s, q, u).start()
-        c_copy(s, q, u).start()
+        if s == 0:
+            x_copy(s, q, u).start()
+            c_copy(s, q, u).start()
 
     for u in range(2):
         for s in range(2):
@@ -240,11 +241,6 @@
     count = length // step
     for i in range(count):
         attend(i)
-        if i == count // 2 - 1:
-            for u in range(2):
-                for s in range(2):
-                    y_copy(s, 1 - s, u).wait_recv()
-                    arrived(s, 1 - s, u)
 
     def crossed(s, q, u):
         x_copy(s, q, u).wait_recv()
@@ -256,20 +252,21 @@
     proj_copy(10, group_of(x + 2, core) + half_group, half_group, other_core).start()
     for u in range(2):
         for s in range(2):
-            crossed(s, s, u)
+            y_copy(s, 1 - s, u).wait_recv()
+            arrived(s, 1 - s, u)
     for u in range(2):
-        for s in range(2):
-            crossed(s, 1 - s, u)
-
-    for s in range(2):
-        for q in range(4):
-            for u in range(2):
-                c_copy(s, q, u).wait()
+        crossed(0, 0, u)
+    for u in range(2):
+        crossed(0, 1, u)
+
+    for q in range(4):
+        for u in range(2):
+            c_copy(0, q, u).wait()
     for u in range(2):
         for q in range(2):
             for s in range(2):
                 y_copy(s, q, u).wait_send()
-                x_copy(s, q, u).wait_send()
+            x_copy(0, q, u).wait_send()
     proj_copy(0, 0, size_z - 1, up_y).wait_send()
     proj_copy(1, 0, (size_y - 1) * size_z, up_y).wait_send()
     for n, amount in ((2, group), (3, group), (5, half_group), (6, half_group)):
@@ -314,10 +311,10 @@
             dma((2,)),
             dma((8,)),
             dma((8,)),
+            dma((4,)),
+            dma((4,)),
             dma((8,)),
             dma((8,)),
-            dma((16,)),
-            dma((16,)),
             dma((11,)),
             dma((11,)),
         ],
@@ -330,7 +327,7 @@
 
 def moe_kernel(axis_size, x_ref, hid_ref, wt_ref, own_g, own_u, own_d, others,
                out_ref, xbuf, acc, act, weights, rbuf, lbuf, start_sem, send_sem, recv_sem, wsem,
-               fsend, frecv, xsend, xrecv, csend, crecv):
+               fsend, frecv, xsend, xrecv, csend, crecv, lsem):
     n = axis_size
     half_n = n // 2
     y, z = lax.axis_index("y"), lax.axis_index("z")
@@ -349,8 +346,8 @@
 
     for i, own in enumerate((own_g, own_u, own_d)):
         pltpu.make_async_copy(own, weights.at[0, i], wsem.at[0]).start()
-    last = count - 1
-    for k in range(1, last):
+    first_late = count - 2
+    for k in range(1, first_late):
         pltpu.make_async_copy(others.at[k - 1], weights.at[k], wsem.at[k]).start()
 
     size_x, size_y = lax.axis_size("x"), lax.axis_size("y")
@@ -397,6 +394,7 @@
             gather_copy(j, way).start()
 
     high, wide = ff // size_x, width // 4
+    near, far_k = count - 2, count - 1
 
     def section(ref, k, q, u):
         columns = pl.ds(pl.multiple_of((core * 2 + u) * wide, wide), wide)
@@ -407,36 +405,45 @@
             src_ref=src, dst_ref=dst, send_sem=send, recv_sem=recv, device_id=device, device_id_type=MESH
         )
 
+    def origin(k, q, u):
+        return section(others, 1, q, u) if k == near and q < 2 else section(weights, k, q, u)
+
     def f_copy(q, u):
         n = q * 2 + u
         return remote(
-            section(others, q, q, u), section(weights, last, q, u), fsend.at[n], frecv.at[n],
+            section(others, q, q, u), section(weights, far_k, q, u), fsend.at[n], frecv.at[n],
             up_y if q == 0 else down_y,
         )
 
-    def x_copy(q, u):
-        n = q * 2 + u
+    def x_copy(k, q, u):
+        n = ((k - near) * 2 + q) * 2 + u
         device, slot = (up_x, 3) if q == 0 else (down_x, 2)
-        return remote(section(weights, last, q, u), section(weights, last, slot, u), xsend.at[n], xrecv.at[n], device)
-
-    def c_copy(q, u):
-        n = q * 2 + u
-        return remote(section(weights, last, q, u), section(weights, last, q, u), csend.at[n], crecv.at[n], other_core)
+        return remote(origin(k, q, u), section(weights, k, slot, u), xsend.at[n], xrecv.at[n], device)
+
+    def c_copy(k, q, u):
+        n = ((k - near) * 4 + q) * 2 + u
+        return remote(origin(k, q, u), section(weights, k, q, u), csend.at[n], crecv.at[n], other_core)
+
+    def local_copy(q, u):
+        return pltpu.make_async_copy(section(others, 1, q, u), section(weights, near, q, u), lsem.at[q * 2 + u])
 
     def arrived(u):
         for q in range(2):
             f_copy(q, u).wait_recv()
-            x_copy(q, u).start()
-            c_copy(q, u).start()
-
-    def crossed(u):
+            x_copy(far_k, q, u).start()
+            c_copy(far_k, q, u).start()
+
+    def crossed(k, u):
         for q in range(2):
-            x_copy(q, u).wait_recv()
-            c_copy(3 if q == 0 else 2, u).start()
+            x_copy(k, q, u).wait_recv()
+            c_copy(k, 3 if q == 0 else 2, u).start()
 
     for u in range(2):
         for q in range(2):
             f_copy(q, u).start()
+            x_copy(near, q, u).start()
+            c_copy(near, q, u).start()
+            local_copy(q, u).start()
 
     def pass_on(j):
         for way in range(2):
@@ -498,9 +505,10 @@
 
         return carry
 
-    early = tuple(range(last))
-    lax.fori_loop(0, last, own_step, 0)
+    early, late = tuple(range(near)), (near, far_k)
+    lax.fori_loop(0, near, own_step, 0)
     down([z], early, False)
+    crossed(near, 0)
     arrived(0)
 
     def pair_step(p, carry):
@@ -516,20 +524,21 @@
 
             return inner
 
-        lax.fori_loop(0, last, one, 0)
+        lax.fori_loop(0, near, one, 0)
         down(slots, early, False)
 
         @pl.when(p == 1)
         def _():
+            crossed(near, 1)
             arrived(1)
 
         @pl.when(p == 2)
         def _():
-            crossed(0)
+            crossed(far_k, 0)
 
         @pl.when(p == 3)
         def _():
-            crossed(1)
+            crossed(far_k, 1)
 
         return carry
 
@@ -540,17 +549,24 @@
         gate_up(far, k)
         return carry
 
-    lax.fori_loop(0, last, far_step, 0)
+    lax.fori_loop(0, near, far_step, 0)
     down(far, early, False)
     for q in range(4):
         for u in range(2):
-            c_copy(q, u).wait_recv()
-
-    def finish(slots):
-        gate_up(slots, last)
-        down(slots, (last,), True)
-
-    finish(far)
+            c_copy(near, q, u).wait_recv()
+            if q < 2:
+                local_copy(q, u).wait()
+
+    def finish(slots, ready=True):
+        gate_up(slots, near)
+        if not ready:
+            for q in range(4):
+                for u in range(2):
+                    c_copy(far_k, q, u).wait_recv()
+        gate_up(slots, far_k)
+        down(slots, late, True)
+
+    finish(far, False)
     bufs = (rbuf, lbuf)
 
     def sum_copy(j, way):
@@ -596,12 +612,14 @@
         for way in range(2):
             gather_copy(j, way).wait_send()
             sum_copy(j, way).wait_send()
-    for q in range(4):
-        for u in range(2):
-            c_copy(q, u).wait_send()
-            if q < 2:
-                f_copy(q, u).wait_send()
-                x_copy(q, u).wait_send()
+    for u in range(2):
+        for k in late:
+            for q in range(4):
+                c_copy(k, q, u).wait_send()
+            for q in range(2):
+                x_copy(k, q, u).wait_send()
+        for q in range(2):
+            f_copy(q, u).wait_send()
 
 
 def mix_experts(normed, hidden, weight_table, own_weights, other_weights):
@@ -628,9 +646,7 @@
             pltpu.SemaphoreType.DMA((2, 2 * sent)),
             pltpu.SemaphoreType.DMA((2, 2 * sent)),
             pltpu.SemaphoreType.DMA((count,)),
-        ] + [pltpu.SemaphoreType.DMA((4,))] * 4 + [
-            pltpu.SemaphoreType.DMA((8,)),
-            pltpu.SemaphoreType.DMA((8,)),
+        ] + [pltpu.SemaphoreType.DMA((amount,)) for amount in (4, 4, 8, 8, 16, 16, 4)] + [
         ],
         compiler_params=pltpu.CompilerParams(
             collective_id=0, has_side_effects=True, vmem_limit_bytes=66000000

time: 259 us -> 261 us (level); the launches traced: 259 us -> 257 us
    pallas_call x1, Pallas kernels: 135 us -> 131 us  [attend_and_gather(): pl.pallas_call(front_kernel, out_shape=(jax.ShapeDtypeStruct((peers // he...]
where the time goes in v5:
time: 261 us; the launch traced here: 257 us
  Pallas kernels  238 us (91%)
  local copies, waits for them, and re-layouts  9.68 us (4%)
  matrix products  4.81 us (2%)
  other arithmetic  3.64 us (1%)
    pallas_call x1, Pallas kernels, attend_and_gather(): pl.pallas_call(front_kernel, out_shape=(jax.ShapeDtypeStruct((peers // he...  131 us
    pallas_call x1, Pallas kernels, mix_experts(): pl.pallas_call(functools.partial(moe_kernel, n), out_shape=jax.ShapeDtype...  108 us

profile of v5, /device:TPU:2, one launch (start us, length us, event | category | flops | bytes accessed | tf_op | source)
XLA Modules:
  0.0 256.7 jit_solution(8535544935016584724)
XLA Ops:
  0.0 0.0 copy-start.4
  0.0 0.0 copy-start.5
  0.0 0.0 copy-start.7
  0.0 0.0 copy-start.8
  0.0 0.0 copy-start
  0.0 0.9 fusion.5
  1.0 0.6 fusion.6
  1.6 2.6 %reshape.39 = bf16[64,32,192]{2,1,0:T(8,128)(2,1)S(1)} reshape(bf16[64,2,3072]{2,1,0:T(2,128)(2,1)} %param.13) | data formatting | bytes 1572864 | tf_op jit(solution)/shard_map/reshape | solution.py:692
  4.2 0.1 slice.9
  4.3 0.2 copy.44
  4.5 0.1 slice.8
  4.6 0.8 copy.36
  5.4 0.1 broadcast_in_dim.27
  5.5 0.5 maximum_bitcast_fusion
  6.0 0.0 copy-done.4
  6.0 0.3 reshape.40
  6.4 0.0 copy-done.5
  6.4 0.3 reshape.41
  6.7 0.4 copy_bitcast_fusion.2
  7.1 0.0 copy-done.7
  7.1 0.1 copy.39
  7.3 0.1 copy.40
  7.3 0.1 broadcast_in_dim.29
  7.4 0.0 copy-done.8
  7.4 0.1 copy.37
  7.5 0.1 copy.38
  7.6 0.1 eq.31
  7.7 0.2 copy.41
  8.0 0.0 copy-done
  8.0 0.0 copy-start.3
  8.0 130.7 %shard_map.127 = (bf16[128,2048]{1,0:T(8,128)(2,1)S(1)}, f32[8,128,4]{2,1,0:T(8,128)S(1)}, bf16[2,3,704,2048]{3,2,1,0:T(8,128)(2,1)}, bf16[256,8,2048]{2,1,0:T(8,128)(2,1)}) custom-call(bf16[32,64,128]{2,1,0:T(8,128)(2,1)S(1)} %get-tuple-element.16.queries, bf16[32,64,128]{2,1,0:T(8,128)(2,1)S(1)} %get-tuple-element.18.keys, ...), custom_call_target="tpu_custom_call" | custom-call | flops 99999997952 | bytes 40000000 | tf_op jit(solution)/shard_map/pallas_call | solution.py:293
  138.7 0.0 copy-start.1
  138.7 0.0 copy-done.3
  138.7 0.6 convert_bitcast_fusion
  139.3 0.6 copy.31
  139.9 0.0 copy-start.6
  140.0 4.8 %multiply_reduce_fusion = (f32[128]{0:T(128)S(1)}, f32[128,2048]{1,0:T(8,128)S(1)}) fusion(f32[128,2048]{1,0:T(8,128)S(1)} %bitcast.45, bf16[128,2048]{1,0:T(8,128)(2,1)S(1)} %get-tuple-element.9, bf16[256,8,2048]{2,1,0:T(8,128)(2,1)} %get-tuple-element.10), kind=kOutput, calls=%fused_computation.5 | convolution fusion | flops 1074528128 | bytes 11010560 | tf_op jit(solution)/shard_map/dot_general | solution.py:716
  144.8 0.0 copy-done.1
  144.8 0.0 copy-start.2
  144.8 0.0 copy-done.6
  144.8 0.9 copy-done.2
  145.7 1.0 multiply_convert_fusion.x_ref
  146.7 107.6 %shard_map.128 = bf16[128,2048]{1,0:T(8,128)(2,1)} custom-call(bf16[128,2048]{1,0:T(8,128)(2,1)} %multiply_convert_fusion.x_ref, f32[128,2048]{1,0:T(8,128)} %copy-done.2, f32[8,128,4]{2,1,0:T(8,128)} %copy-done.1, bf16[704,2048]{1,0:T(8,128)(2,1)} %bitcast.52, bf16[704,2048]{1,0:T(8,128)(2,1)} %bitcast.54, bf16[704,2048]{1,0:T(8,128)(2,1)} %bitcast.56, ...), custom_call_target="tpu_custom_call" | custom-call | flops 35433480192 | bytes 40000000 | tf_op jit(solution)/shard_map/pallas_call | solution.py:633
  254.3 2.4 copy.49
  (3 shorter events, 0.0 us)
Async XLA Ops:
  0.0 6.0 %copy-start.4 = (bf16[64,2,2048]{2,1,0:T(2,128)(2,1)S(1)}, bf16[64,2,2048]{2,1,0:T(2,128)(2,1)}, u32[]{:S(2)}) copy-start(bf16[64,2,2048]{2,1,0:T(2,128)(2,1)} %param.14) | copy-start | bytes 1572868
  0.0 6.4 %copy-start.5 = (bf16[64,2,2048]{2,1,0:T(2,128)(2,1)S(1)}, bf16[64,2,2048]{2,1,0:T(2,128)(2,1)}, u32[]{:S(2)}) copy-start(bf16[64,2,2048]{2,1,0:T(2,128)(2,1)} %param.16) | copy-start | bytes 1572868
  0.0 7.1 %copy-start.7 = (f32[1,1,128,6]{2,1,3,0:T(1,128)S(1)}, f32[1,1,128,6]{2,1,3,0:T(1,128)}, u32[]{:S(2)}) copy-start(f32[1,1,128,6]{2,1,3,0:T(1,128)} %param.25) | copy-start | bytes 9220
  0.0 7.4 %copy-start.8 = (s32[1,1,128,6]{2,1,3,0:T(1,128)S(1)}, s32[1,1,128,6]{2,1,3,0:T(1,128)}, u32[]{:S(2)}) copy-start(s32[1,1,128,6]{2,1,3,0:T(1,128)} %param.24) | copy-start | bytes 9220
  0.0 8.0 %copy-start = (bf16[8,2048]{1,0:T(8,128)(2,1)S(1)}, bf16[8,2048]{1,0:T(8,128)(2,1)}, u32[]{:S(2)}) copy-start(bf16[8,2048]{1,0:T(8,128)(2,1)} %proj.1) | copy-start | bytes 98308
  8.0 130.7 %copy-start.3 = (bf16[64,2,2048]{2,1,0:T(2,128)(2,1)S(1)}, bf16[64,2,2048]{2,1,0:T(2,128)(2,1)}, u32[]{:S(2)}) copy-start(bf16[64,2,2048]{2,1,0:T(2,128)(2,1)} %param.17) | copy-start | bytes 1572868
  138.7 6.1 %copy-start.1 = (f32[8,128,4]{2,1,0:T(8,128)}, f32[8,128,4]{2,1,0:T(8,128)S(1)}, u32[]{:S(2)}) copy-start(f32[8,128,4]{2,1,0:T(8,128)S(1)} %get-tuple-element.11.wt_ref) | copy-start | bytes 49156
  139.9 4.9 %copy-start.6 = (bf16[2048]{0:T(1024)(128)(2,1)S(1)}, bf16[2048]{0:T(1024)(128)(2,1)}, u32[]{:S(2)}) copy-start(bf16[2048]{0:T(1024)(128)(2,1)} %param.20) | copy-start | bytes 12292
  144.8 1.0 copy-start.2

commit v6 on v5

--- a/solution.py
+++ b/solution.py
@@ -153,18 +153,9 @@
             x_copy(s, q, u).start()
             c_copy(s, q, u).start()
 
-    for u in range(2):
-        for s in range(2):
-            y_copy(s, s, u).wait_recv()
-            arrived(s, s, u)
-
-    half_group = group // 2
-    proj_copy(2, group_of(x - 1, core), group, up_x).wait_recv()
-    proj_copy(5, group_of(x - 1, core), half_group, up_x).start()
-    proj_copy(7, group_of(x - 1, core), group, other_core).start()
-    proj_copy(3, group_of(x + 1, core), group, up_x).wait_recv()
-    proj_copy(6, group_of(x + 1, core) + half_group, half_group, down_x).start()
-    proj_copy(8, group_of(x + 1, core), group, other_core).start()
+    for s in range(2):
+        y_copy(s, s, 0).wait_recv()
+        arrived(s, s, 0)
 
     own_place = rows_buf.at[rows_of(me)]
     pltpu.make_async_copy(own_place, own_place, local_sem.at[0]).wait()
@@ -241,11 +232,23 @@
     count = length // step
     for i in range(count):
         attend(i)
+        if i + 1 != (count + 1) // 2:
+            continue
+        half_group = group // 2
+        proj_copy(2, group_of(x - 1, core), group, up_x).wait_recv()
+        proj_copy(5, group_of(x - 1, core), half_group, up_x).start()
+        proj_copy(7, group_of(x - 1, core), group, other_core).start()
+        proj_copy(3, group_of(x + 1, core), group, up_x).wait_recv()
+        proj_copy(6, group_of(x + 1, core) + half_group, half_group, down_x).start()
+        proj_copy(8, group_of(x + 1, core), group, other_core).start()
 
     def crossed(s, q, u):
         x_copy(s, q, u).wait_recv()
         c_copy(s, 3 if q == 0 else 2, u).start()
 
+    for s in range(2):
+        y_copy(s, s, 1).wait_recv()
+        arrived(s, s, 1)
     proj_copy(5, 0, half_group, up_x).wait_recv()
     proj_copy(9, group_of(x + 2, core), half_group, other_core).start()
     proj_copy(6, 0, half_group, up_x).wait_recv()

time: 261 us -> 250 us (0.958)
  Pallas kernels: 238 us -> 229 us
    pallas_call x1, Pallas kernels: 131 us -> 122 us  [attend_and_gather(): pl.pallas_call(front_kernel, out_shape=(jax.ShapeDtypeStruct((peers // he...]
where the time goes in v6:
time: 250 us; the launch traced here: 248 us
  Pallas kernels  229 us (92%)
  local copies, waits for them, and re-layouts  9.68 us (4%)
  matrix products  4.8 us (2%)
  other arithmetic  3.64 us (1%)
    pallas_call x1, Pallas kernels, attend_and_gather(): pl.pallas_call(front_kernel, out_shape=(jax.ShapeDtypeStruct((peers // he...  122 us
    pallas_call x1, Pallas kernels, mix_experts(): pl.pallas_call(functools.partial(moe_kernel, n), out_shape=jax.ShapeDtype...  107 us

profile of v6, /device:TPU:2, one launch (start us, length us, event | category | flops | bytes accessed | tf_op | source)
XLA Modules:
  0.0 247.7 jit_solution(10764421122203026889)
XLA Ops:
  0.0 0.0 copy-start.4
  0.0 0.0 copy-start.5
  0.0 0.0 copy-start.7
  0.0 0.0 copy-start.8
  0.0 0.0 copy-start
  0.0 0.9 fusion.5
  1.0 0.6 fusion.6
  1.6 2.6 %reshape.39 = bf16[64,32,192]{2,1,0:T(8,128)(2,1)S(1)} reshape(bf16[64,2,3072]{2,1,0:T(2,128)(2,1)} %param.13) | data formatting | bytes 1572864 | tf_op jit(solution)/shard_map/reshape | solution.py:695
  4.2 0.1 slice.9
  4.3 0.2 copy.44
  4.5 0.1 slice.8
  4.6 0.8 copy.36
  5.4 0.1 broadcast_in_dim.27
  5.5 0.5 maximum_bitcast_fusion
  6.0 0.0 copy-done.4
  6.0 0.3 reshape.40
  6.4 0.0 copy-done.5
  6.4 0.3 reshape.41
  6.7 0.4 copy_bitcast_fusion.2
  7.1 0.0 copy-done.7
  7.1 0.1 copy.39
  7.3 0.1 copy.40
  7.3 0.1 broadcast_in_dim.29
  7.4 0.0 copy-done.8
  7.4 0.1 copy.37
  7.5 0.1 copy.38
  7.6 0.1 eq.31
  7.7 0.2 copy.41
  8.0 0.0 copy-done
  8.0 0.0 copy-start.3
  8.0 122.1 %shard_map.127 = (bf16[128,2048]{1,0:T(8,128)(2,1)S(1)}, f32[8,128,4]{2,1,0:T(8,128)S(1)}, bf16[2,3,704,2048]{3,2,1,0:T(8,128)(2,1)}, bf16[256,8,2048]{2,1,0:T(8,128)(2,1)}) custom-call(bf16[32,64,128]{2,1,0:T(8,128)(2,1)S(1)} %get-tuple-element.16.queries, bf16[32,64,128]{2,1,0:T(8,128)(2,1)S(1)} %get-tuple-element.18.keys, ...), custom_call_target="tpu_custom_call" | custom-call | flops 99999997952 | bytes 40000000 | tf_op jit(solution)/shard_map/pallas_call | solution.py:296
  130.1 0.0 copy-start.1
  130.1 0.0 copy-done.3
  130.1 0.6 convert_bitcast_fusion
  130.7 0.6 copy.31
  131.3 0.0 copy-start.6
  131.3 4.8 %multiply_reduce_fusion = (f32[128]{0:T(128)S(1)}, f32[128,2048]{1,0:T(8,128)S(1)}) fusion(f32[128,2048]{1,0:T(8,128)S(1)} %bitcast.45, bf16[128,2048]{1,0:T(8,128)(2,1)S(1)} %get-tuple-element.9, bf16[256,8,2048]{2,1,0:T(8,128)(2,1)} %get-tuple-element.10), kind=kOutput, calls=%fused_computation.5 | convolution fusion | flops 1074528128 | bytes 11010560 | tf_op jit(solution)/shard_map/dot_general | solution.py:719
  136.1 0.0 copy-done.1
  136.2 0.0 copy-start.2
  136.2 0.0 copy-done.6
  136.2 0.9 copy-done.2
  137.1 1.0 multiply_convert_fusion.x_ref
  138.1 107.2 %shard_map.128 = bf16[128,2048]{1,0:T(8,128)(2,1)} custom-call(bf16[128,2048]{1,0:T(8,128)(2,1)} %multiply_convert_fusion.x_ref, f32[128,2048]{1,0:T(8,128)} %copy-done.2, f32[8,128,4]{2,1,0:T(8,128)} %copy-done.1, bf16[704,2048]{1,0:T(8,128)(2,1)} %bitcast.52, bf16[704,2048]{1,0:T(8,128)(2,1)} %bitcast.54, bf16[704,2048]{1,0:T(8,128)(2,1)} %bitcast.56, ...), custom_call_target="tpu_custom_call" | custom-call | flops 35433480192 | bytes 40000000 | tf_op jit(solution)/shard_map/pallas_call | solution.py:636
  245.3 2.4 copy.49
  (3 shorter events, 0.0 us)
Async XLA Ops:
  0.0 6.0 %copy-start.4 = (bf16[64,2,2048]{2,1,0:T(2,128)(2,1)S(1)}, bf16[64,2,2048]{2,1,0:T(2,128)(2,1)}, u32[]{:S(2)}) copy-start(bf16[64,2,2048]{2,1,0:T(2,128)(2,1)} %param.14) | copy-start | bytes 1572868
  0.0 6.4 %copy-start.5 = (bf16[64,2,2048]{2,1,0:T(2,128)(2,1)S(1)}, bf16[64,2,2048]{2,1,0:T(2,128)(2,1)}, u32[]{:S(2)}) copy-start(bf16[64,2,2048]{2,1,0:T(2,128)(2,1)} %param.16) | copy-start | bytes 1572868
  0.0 7.1 %copy-start.7 = (f32[1,1,128,6]{2,1,3,0:T(1,128)S(1)}, f32[1,1,128,6]{2,1,3,0:T(1,128)}, u32[]{:S(2)}) copy-start(f32[1,1,128,6]{2,1,3,0:T(1,128)} %param.25) | copy-start | bytes 9220
  0.0 7.4 %copy-start.8 = (s32[1,1,128,6]{2,1,3,0:T(1,128)S(1)}, s32[1,1,128,6]{2,1,3,0:T(1,128)}, u32[]{:S(2)}) copy-start(s32[1,1,128,6]{2,1,3,0:T(1,128)} %param.24) | copy-start | bytes 9220
  0.0 8.0 %copy-start = (bf16[8,2048]{1,0:T(8,128)(2,1)S(1)}, bf16[8,2048]{1,0:T(8,128)(2,1)}, u32[]{:S(2)}) copy-start(bf16[8,2048]{1,0:T(8,128)(2,1)} %proj.1) | copy-start | bytes 98308
  8.0 122.1 %copy-start.3 = (bf16[64,2,2048]{2,1,0:T(2,128)(2,1)S(1)}, bf16[64,2,2048]{2,1,0:T(2,128)(2,1)}, u32[]{:S(2)}) copy-start(bf16[64,2,2048]{2,1,0:T(2,128)(2,1)} %param.17) | copy-start | bytes 1572868
  130.1 6.1 %copy-start.1 = (f32[8,128,4]{2,1,0:T(8,128)}, f32[8,128,4]{2,1,0:T(8,128)S(1)}, u32[]{:S(2)}) copy-start(f32[8,128,4]{2,1,0:T(8,128)S(1)} %get-tuple-element.11.wt_ref) | copy-start | bytes 49156
  131.3 4.8 %copy-start.6 = (bf16[2048]{0:T(1024)(128)(2,1)S(1)}, bf16[2048]{0:T(1024)(128)(2,1)}, u32[]{:S(2)}) copy-start(bf16[2048]{0:T(1024)(128)(2,1)} %param.20) | copy-start | bytes 12292
  136.2 1.0 copy-start.2
